TPU v7x, 128 devices: a whole 4x4x4 slice. The times are simulated.
128 devices in a mesh: scale: 2 (over y_hi), lat: 64 (over x, z, y_lo, core).
Axes of the slice: x: 4, y: 4 (y_hi: 2, y_lo: 2; y = y_hi * 2 + y_lo), z: 4, core: 2. Of those that a mesh axis runs over, the one named last changes fastest.
Arguments:
- fine_state: float32 [64, 2, 1280, 1280], P(None, None, ('scale', 'lat')), may hold values from -6 to 6
- fine_noise: bfloat16 [64, 2, 1280, 1280], P(None, None, ('scale', 'lat')), may hold values from -6 to 6
- medium_state: float32 [64, 2, 640, 640], P(None, None, ('scale', 'lat')), may hold values from -6 to 6
- medium_noise: bfloat16 [64, 2, 640, 640], P(None, None, ('scale', 'lat')), may hold values from -6 to 6
- coarse_state: float32 [64, 2, 160, 160], P('lat'), may hold values from -6 to 6
- coarse_noise: bfloat16 [64, 2, 160, 160], P('lat'), may hold values from -6 to 6
- decay: float32 [3], replicated, may hold values from 0.5 to 0.95
- amplitude: float32 [3], replicated, may hold values from 0.3 to 1
- fine_basis: bfloat16 [1280, 128, 1280], P(('scale', 'lat')), may hold values from -0.0017089844 to 0.0017089844
- medium_basis: bfloat16 [640, 128, 640], P(('scale', 'lat')), may hold values from -0.0034179688 to 0.0034179688
- coarse_basis: bfloat16 [128, 160, 160], P(('scale', 'lat')), may hold values from -0.013671875 to 0.013671875
Outputs:
- fine_next: float32 [64, 2, 1280, 1280], P(None, None, ('scale', 'lat'))
- medium_next: float32 [64, 2, 640, 640], P(None, None, ('scale', 'lat'))
- coarse_next: float32 [64, 2, 160, 160], P('lat')
- pattern: float32 [64, 128, 2560], P(None, ('scale', 'lat'))
All inputs are finite; a program needn't handle non-finite values.
Results may differ from a plain program's by a relative error of at most 0.005.
Values may be sent and summed in bfloat16 or wider, within the bound.
A program may use at most 128 MiB of HBM per device.

v0:
```python
import math

import jax
import jax.numpy as jnp
from jax import lax
from jax.sharding import PartitionSpec as P

NLON = 2560


def advance(state, noise, decay_rate, amp_rate, offset):
    slots = state.shape[3]
    mode_ids = offset + jnp.arange(state.shape[2], dtype=jnp.int32)
    degree_ids = jnp.arange(slots, dtype=jnp.int32)
    inside = mode_ids[:, None] + degree_ids[None, :] < slots
    updated = decay_rate * state + amp_rate * noise.astype(jnp.float32)
    return jnp.where(inside, updated, jnp.zeros_like(updated))


def grid_table(mode_ids):
    lon_ids = jnp.arange(NLON, dtype=jnp.int32)
    angles = (mode_ids[:, None] * lon_ids[None, :] % NLON).astype(jnp.float32) * (
        2.0 * math.pi / NLON
    )
    weights = jnp.where(mode_ids == 0, 1.0, 2.0).astype(jnp.float32)[:, None]
    return jnp.stack([weights * jnp.cos(angles), -weights * jnp.sin(angles)]).astype(jnp.bfloat16)


def body(
    fine_state,
    fine_noise,
    medium_state,
    medium_noise,
    coarse_state,
    coarse_noise,
    decay,
    amplitude,
    fine_basis,
    medium_basis,
    coarse_basis,
):
    place = lax.axis_index(("scale", "lat"))
    fine_next = advance(fine_state, fine_noise, decay[0], amplitude[0], place * fine_state.shape[2])
    medium_next = advance(
        medium_state, medium_noise, decay[1], amplitude[1], place * medium_state.shape[2]
    )
    coarse_next = advance(coarse_state, coarse_noise, decay[2], amplitude[2], 0)
    fine_fourier = jnp.einsum(
        "ecmk,mrk->ecmr",
        fine_next.astype(jnp.bfloat16),
        fine_basis,
        preferred_element_type=jnp.float32,
    ).astype(jnp.bfloat16)
    medium_fourier = jnp.einsum(
        "ecmk,mrk->ecmr",
        medium_next.astype(jnp.bfloat16),
        medium_basis,
        preferred_element_type=jnp.float32,
    ).astype(jnp.bfloat16)
    coarse_half = coarse_next.astype(jnp.bfloat16)
    coarse_fourier = jnp.einsum(
        "ecmk,rmk->ecmr",
        lax.all_gather(coarse_half, "lat", axis=0, tiled=True),
        coarse_basis,
        preferred_element_type=jnp.float32,
    ).astype(jnp.bfloat16)
    fine_cols, medium_cols = (
        lax.all_to_all(fine_fourier, ("scale", "lat"), split_axis=3, concat_axis=2, tiled=True),
        lax.all_to_all(medium_fourier, ("scale", "lat"), split_axis=3, concat_axis=2, tiled=True),
    )
    joined = jnp.concatenate([fine_cols, medium_cols, coarse_fourier], axis=2)
    joined_ids = jnp.concatenate(
        [
            jnp.arange(fine_cols.shape[2], dtype=jnp.int32),
            jnp.arange(medium_cols.shape[2], dtype=jnp.int32),
            jnp.arange(coarse_fourier.shape[2], dtype=jnp.int32),
        ]
    )
    table = grid_table(joined_ids)
    total = jnp.einsum("ecmr,cml->erl", joined, table, preferred_element_type=jnp.float32)
    pattern = jnp.tanh(total)
    return (fine_next, medium_next, coarse_next, pattern)


def solution(mesh):
    return jax.shard_map(
        body,
        mesh=mesh,
        in_specs=(
            P(None, None, ("scale", "lat"), None),
            P(None, None, ("scale", "lat"), None),
            P(None, None, ("scale", "lat"), None),
            P(None, None, ("scale", "lat"), None),
            P("lat", None, None, None),
            P("lat", None, None, None),
            P(),
            P(),
            P(("scale", "lat"), None, None),
            P(("scale", "lat"), None, None),
            P(("scale", "lat"), None, None),
        ),
        out_specs=(
            P(None, None, ("scale", "lat"), None),
            P(None, None, ("scale", "lat"), None),
            P("lat", None, None, None),
            P(None, ("scale", "lat"), None),
        ),
        check_vma=False,
    )
```

profile of v0, /device:TPU:1, one launch (start us, length us, event | category | flops | bytes accessed | tf_op | source)
XLA Modules:
  0.0 183.9 jit_solution(13842432623820553434)
XLA Ops:
  7.2 0.0 copy-start
  7.2 0.0 all-gather.2.cloned.1.call-start
  7.3 1.4 fusion.47
  8.7 1.4 fusion.48
  10.1 3.2 %fusion.46 = (bf16[1,2,160,160]{3,2,1,0:T(8,128)(2,1)}, f32[1,2,160,160]{3,2,1,0:T(8,128)}) fusion(bf16[1,2,160,160]{3,2,1,0:T(8,128)(2,1)} %param.16, f32[]{:T(128)} %bitcast.5, f32[1,2,160,160]{3,2,1,0:T(8,128)} %param.15, f32[]{:T(128)} %bitcast.4, pred[160,160]{1,0:T(8,128)(4,1)S(1)} %add_compare_fusion), kind=kLoop, calls=%fused_computation.49 | loop fusion | flops 307200 | bytes 640008 | tf_op jit(solution)/shard_map/convert_element_type | solution.py:60
  13.3 0.0 all-gather.2.cloned.1.call-update
  13.3 0.1 add_compare_fusion.2
  13.4 5.4 %fusion.45 = (bf16[64,2,5,640]{3,1,2,0:T(2,128)(2,1)S(1)}, f32[64,2,5,640]{3,1,2,0:T(2,128)}) fusion(bf16[64,2,5,640]{3,1,2,0:T(2,128)(2,1)} %param.14, f32[]{:T(128)} %bitcast.3, f32[64,2,5,640]{3,1,2,0:T(2,128)} %param.13, f32[]{:T(128)} %bitcast.2, pred[5,640]{1,0:T(8,128)(4,1)S(1)} %add_compare_fusion.2), kind=kLoop, calls=%fused_computation.48 | loop fusion | flops 2457600 | bytes 4918408 | tf_op jit(solution)/shard_map/convert_element_type | solution.py:56
  18.8 1.6 fusion.33
  20.4 0.9 copy.28
  21.4 1.9 %reshape.180 = bf16[128,2,320]{2,1,0:T(2,128)(2,1)} reshape(bf16[128,5,2,64]{3,2,1,0:T(2,128)(2,1)} %bitcast.62) | data formatting | bytes 327680
  23.3 11.5 %all-to-all-start.1 = ((bf16[128,2,320]{2,1,0:T(2,128)(2,1)}), bf16[128,2,320]{2,1,0:T(2,128)(2,1)S(1)}, u32[]{:S(2)}, u32[]{:S(2)}) async-start(bf16[128,2,320]{2,1,0:T(2,128)(2,1)} %reshape.180), calls=%async_computation.1 | async-start | bytes 393216 | tf_op jit(solution)/shard_map/all_to_all | solution.py:69
  34.8 0.1 add_compare_fusion.1
  34.9 11.3 %fusion.44 = (bf16[64,2,10,1280]{3,1,2,0:T(2,128)(2,1)S(1)}, f32[64,2,10,1280]{3,1,2,0:T(2,128)}) fusion(bf16[64,2,10,1280]{3,1,2,0:T(2,128)(2,1)} %param.12, f32[]{:T(128)} %bitcast.1, f32[64,2,10,1280]{3,1,2,0:T(2,128)} %param.11, f32[]{:T(128)} %bitcast, pred[10,1280]{1,0:T(8,128)(4,1)S(1)} %add_compare_fusion.1), kind=kLoop, calls=%fused_computation.47 | loop fusion | flops 9830400 | bytes 19673608 | tf_op jit(solution)/shard_map/convert_element_type | solution.py:50
  46.2 0.0 copy-done
  46.3 1.7 fusion.28
  48.0 1.4 copy.26
  49.4 1.1 reshape.182
  50.5 0.0 all-to-all-done.1
  50.6 9.8 %all-to-all-start = ((bf16[128,2,640]{2,1,0:T(2,128)(2,1)}), bf16[128,2,640]{2,1,0:T(2,128)(2,1)S(1)}, u32[]{:S(2)}, u32[]{:S(2)}) async-start(bf16[128,2,640]{2,1,0:T(2,128)(2,1)} %reshape.182), calls=%async_computation | async-start | bytes 655360 | tf_op jit(solution)/shard_map/all_to_all | solution.py:68
  60.3 0.0 copy-start.2
  60.3 93.9 %multiply_convert_fusion.1 = (bf16[1,2080,2560]{2,1,0:T(8,128)(2,1)}, bf16[1,2080,2560]{2,1,0:T(8,128)(2,1)}) fusion(s32[2080]{0:T(1024)S(1)} %get-tuple-element.23, f32[2080]{0:T(1024)S(1)} %get-tuple-element.22, f32[2080]{0:T(1024)S(1)} %fusion.43), kind=kLoop, calls=%fused_computation.8 | loop fusion | flops 69222400 | bytes 21324160 | tf_op jit(solution)/shard_map/convert
  154.3 0.3 reshape.181
  154.6 0.2 copy.30
  154.8 0.0 all-to-all-done
  154.8 0.4 reshape.183
  155.2 1.1 copy.29
  156.3 0.0 all-gather.2.cloned.1.call-done
  156.3 0.0 copy-done.2
  156.3 9.7 %fusion.9 = bf16[160,1,64,2]{2,1,3,0:T(2,128)(2,1)S(1)} fusion(bf16[64,2,160,160]{3,2,1,0:T(8,128)(2,1)} %all-gather.2.cloned.1.call-done, bf16[160,160,1,1]{1,0,2,3:T(8,128)(2,1)S(1)} %bitcast.64), kind=kOutput, calls=%fused_computation.13 | convolution fusion | flops 6553600 | bytes 6645760 | tf_op jit(solution)/shard_map/ecmk,rmk->ecmr/dot_general | solution.py:61
  165.9 0.1 copy.36
  166.1 0.0 copy-start.1
  166.1 9.5 %fusion.17 = f32[64,1,2560]{2,0,1:T(8,128)S(1)} fusion(bf16[1,2080,2560]{2,1,0:T(8,128)(2,1)} %get-tuple-element.25, bf16[1,2080,2560]{2,1,0:T(8,128)(2,1)} %get-tuple-element.24, bf16[64,2,160,1]{2,0,1,3:T(8,128)(2,1)S(1)} %fusion.41, bf16[64,2,640,1]{2,0,1,3:T(8,128)(2,1)S(1)} %copy.30, bf16[64,2,1280,1]{2,0,1,3:T(8,128)(2,1)} %copy.29), kind=kOutput, calls=%fused_computation.18 | convolution fusion | flops 1375395840 | bytes 22487040 | tf_op jit(solution)/shard_map/ecmr,cml->erl/dot_general | solution.py:80
  175.6 1.5 copy.31
  177.1 0.0 copy-done.1
  (9 shorter events, 0.1 us)
Async XLA Ops:
  7.2 39.1 %copy-start = (bf16[10,128,1280]{2,1,0:T(8,128)(2,1)S(1)}, bf16[10,128,1280]{2,1,0:T(8,128)(2,1)}, u32[]{:S(2)}) copy-start(bf16[10,128,1280]{2,1,0:T(8,128)(2,1)} %param.19) | copy-start | bytes 9830404
  7.2 149.1 %all-gather.2.cloned.1.call-start = ((), (), s32[]{:S(2)}) async-start(), calls=%async_computation.2 | async-start | bytes 10649600 | tf_op jit(solution)/shard_map/all_gather | solution.py:63
  23.3 27.2 %all-to-all-start.1 = ((bf16[128,2,320]{2,1,0:T(2,128)(2,1)}), bf16[128,2,320]{2,1,0:T(2,128)(2,1)S(1)}, u32[]{:S(2)}, u32[]{:S(2)}) async-start(bf16[128,2,320]{2,1,0:T(2,128)(2,1)} %reshape.180), calls=%async_computation.1 | async-start | bytes 393216 | tf_op jit(solution)/shard_map/all_to_all | solution.py:69
  50.6 104.2 %all-to-all-start = ((bf16[128,2,640]{2,1,0:T(2,128)(2,1)}), bf16[128,2,640]{2,1,0:T(2,128)(2,1)S(1)}, u32[]{:S(2)}, u32[]{:S(2)}) async-start(bf16[128,2,640]{2,1,0:T(2,128)(2,1)} %reshape.182), calls=%async_computation | async-start | bytes 655360 | tf_op jit(solution)/shard_map/all_to_all | solution.py:68
  60.3 95.9 %copy-start.2 = (bf16[1,160,160]{2,1,0:T(8,128)(2,1)S(1)}, bf16[1,160,160]{2,1,0:T(8,128)(2,1)}, u32[]{:S(2)}) copy-start(bf16[1,160,160]{2,1,0:T(8,128)(2,1)} %param.21) | copy-start | bytes 153604
  166.1 11.0 %copy-start.1 = (bf16[10,128,1280]{2,1,0:T(8,128)(2,1)S(1)}, bf16[10,128,1280]{2,1,0:T(8,128)(2,1)}, u32[]{:S(2)}) copy-start(bf16[10,128,1280]{2,1,0:T(8,128)(2,1)} %param.19) | copy-start | bytes 9830404
Sparse Core Ops, SparseCore 0:
  13.4 120.2 all-gather.1
where the time goes:
time: 185 us; the launch traced here: 184 us
  other arithmetic  114 us (62%)
  matrix products  22.5 us (12%)
  starting transfers between devices  21.3 us (12%)
  between operations  14.2 us (8%)
  local copies, waits for them, and re-layouts  11.8 us (6%)
    another operation x1, other arithmetic  93.9 us
    all_to_all x1, starting transfers between devices, body(): lax.all_to_all(medium_fourier, ('scale', 'lat'), split_axis=3, concat_axi...  11.5 us
    convert_element_type x1, other arithmetic, body(): fine_next.astype(jnp.bfloat16)  11.3 us
    all_to_all x1, starting transfers between devices, body(): lax.all_to_all(fine_fourier, ('scale', 'lat'), split_axis=3, concat_axis=...  9.77 us
    dot_general x1, matrix products, body(): jnp.einsum('ecmk,rmk->ecmr', lax.all_gather(coarse_half, 'lat', axis=0, t...  9.65 us
    dot_general x1, matrix products, body(): jnp.einsum('ecmr,cml->erl', joined, table, preferred_element_type=jnp.flo...  9.48 us
    convert_element_type x1, other arithmetic, body(): medium_next.astype(jnp.bfloat16)  5.45 us
    unnamed x11, local copies, waits for them, and re-layouts  5.29 us
  transfers between devices with their start and end apart: 3, of which 0 were waited for; matrix products, arithmetic and copies ran while one was open for 66% of the time, Pallas kernels for 0%

commit v1 on v0

v1 whole, which is shorter than its diff:
```python
import math

import jax
import jax.numpy as jnp
import numpy as np
from jax import lax
from jax.experimental import pallas as pl
from jax.experimental.pallas import tpu as pltpu
from jax.sharding import PartitionSpec as P

MESH = pl.DeviceIdType.MESH
F32, BF16 = jnp.float32, jnp.bfloat16
ANY = pl.BlockSpec(memory_space=pl.ANY)
HBM = pl.BlockSpec(memory_space=pltpu.HBM)
VMEM = pl.BlockSpec(memory_space=pltpu.VMEM)
SMEM = pl.BlockSpec(memory_space=pltpu.SMEM)
MF, MM, MC, NLON, NE, NR = 1280, 640, 160, 2560, 64, 128
ND = 128
OWNERS = 32
TWO_TILES = 7
NT = (((1,), (1,)), ((), ()))


def my_place():
    return lax.axis_index("scale") * 64 + lax.axis_index("lat")


def to_device(d):
    return (d // 64, d % 64)


def coarse_kernel(cs, cn, cb, dec, amp, nxt, h0, h1, b0, b1, pad, bpad):
    scale = lax.axis_index("scale")
    deg = lax.broadcasted_iota(jnp.int32, (MC, MC), 0) + lax.broadcasted_iota(jnp.int32, (MC, MC), 1)
    for c in range(2):
        val = dec[2] * cs[0, c] + amp[2] * cn[0, c].astype(F32)
        val = jnp.where(deg < MC, val, 0.0)
        nxt[0, c] = val
    pad[pl.ds(160, 8), :] = jnp.zeros((8, 256), F32)
    bpad[pl.ds(160, 8), :] = jnp.zeros((8, 256), F32)
    pad[pl.ds(0, 160), pl.ds(128, 128)] = jnp.zeros((160, 128), F32)
    bpad[pl.ds(0, 160), pl.ds(128, 128)] = jnp.zeros((160, 128), F32)
    pad[pl.ds(0, 160), pl.ds(0, 160)] = nxt[0, scale]
    bpad[pl.ds(0, 160), pl.ds(0, 160)] = cb[0].astype(F32)
    for p in range(OWNERS):
        h0[p] = pad[pl.ds(5 * p, 8), pl.ds(0, 128)].astype(BF16)
        b0[p] = bpad[pl.ds(5 * p, 8), pl.ds(0, 128)].astype(BF16)
        if p < TWO_TILES:
            h1[p] = pad[pl.ds(5 * p, 8), pl.ds(128, 128)].astype(BF16)
            b1[p] = bpad[pl.ds(5 * p, 8), pl.ds(128, 128)].astype(BF16)


def coarse_call(cs, cn, cb, dec, amp):
    s = jax.ShapeDtypeStruct
    return pl.pallas_call(
        coarse_kernel,
        name="coarse_advance",
        out_shape=(
            s((1, 2, MC, MC), F32),
            s((OWNERS, 8, 128), BF16),
            s((TWO_TILES, 8, 128), BF16),
            s((OWNERS, 8, 128), BF16),
            s((TWO_TILES, 8, 128), BF16),
        ),
        in_specs=[VMEM, VMEM, VMEM, SMEM, SMEM],
        out_specs=(VMEM,) * 5,
        scratch_shapes=[pltpu.VMEM((168, 256), F32), pltpu.VMEM((168, 256), F32)],
        cost_estimate=pl.CostEstimate(flops=10**6, bytes_accessed=10**6, transcendentals=0),
    )(cs, cn, cb, dec, amp)


def reshard_kernel(h0, h1, b0, b1, rh0, rh1, rb0, rb1, send, recv_h, recv_b, here):
    me = my_place()

    def go(i, tops, k, sent):
        p = lax.rem(me + i, tops)
        tiles = ((h0, rh0, recv_h), (b0, rb0, recv_b)) if k == 0 else ((h1, rh1, recv_h), (b1, rb1, recv_b))

        @pl.when(p != me)
        def _():
            for src, dst, sem in tiles:
                pltpu.make_async_remote_copy(
                    src.at[p], dst.at[me], send.at[k], sem.at[k], device_id=to_device(p), device_id_type=MESH
                ).start()

        @pl.when(p == me)
        def _():
            for src, dst, _ in tiles:
                pltpu.make_async_copy(src.at[p], dst.at[me], here.at[k]).start()

    @pl.loop(0, OWNERS)
    def _(i):
        go(i, OWNERS, 0, send)

    @pl.loop(0, TWO_TILES)
    def _(i):
        go(i, TWO_TILES, 1, send)

    def wait(count, sem):
        part = rh0.at[pl.ds(0, count)]
        pltpu.make_async_copy(part, part, sem).wait()

    for k, tops in ((0, OWNERS), (1, TWO_TILES)):

        @pl.when(me < tops)
        def _():
            wait(2 * tops - 2, send.at[k])
            wait(2, here.at[k])
            wait(ND - 1, recv_h.at[k])
            wait(ND - 1, recv_b.at[k])

        @pl.when(me >= tops)
        def _():
            wait(2 * tops, send.at[k])


def reshard_call(h0, h1, b0, b1):
    s = jax.ShapeDtypeStruct((ND, 8, 128), BF16)
    return pl.pallas_call(
        reshard_kernel,
        name="coarse_reshard",
        out_shape=(s, s, s, s),
        in_specs=[HBM] * 4,
        out_specs=(ANY,) * 4,
        scratch_shapes=[pltpu.SemaphoreType.DMA((2,))] * 4,
        compiler_params=pltpu.CompilerParams(has_side_effects=True, vmem_limit_bytes=67_000_000),
        cost_estimate=pl.CostEstimate(flops=10**6, bytes_accessed=10**6, transcendentals=0),
    )(h0, h1, b0, b1)


BLOCKS = [(0, 0), (0, 1), (1, 0), (1, 1), (2, 0)]


def spectral_kernel(
    fs, fn, ms, mn, fb, mb, rh0, rh1, rb0, rb1, dec, amp,
    fo, mo, g,
    s_buf, n_buf, fb_buf, mb_buf, a_buf, acc, gf, c_raw, hf, bf,
    s_sem, n_sem, b_sem, o_sem, c_sem,
):
    me = my_place()
    order = [4, 0, 1, 2, 3]

    def start_copies(u, kt, out):
        grp, q = BLOCKS[u]
        lanes = pl.ds((q * 5 + kt) * 128, 128)
        rows = s_buf.at[u].reshape(5 * 64, 5, 2, 128).at[pl.ds(kt * 64, 64)]
        nrows = n_buf.at[u, pl.ds(kt * 64, 64)]
        if grp == 2:
            src, nsrc, dst = ms, mn, mo
            mid = slice(None)
        else:
            src, nsrc, dst = fs, fn, fo
            mid = pl.ds(grp * 5, 5)
        if out:
            pltpu.make_async_copy(rows, dst.at[:, mid, :, lanes], o_sem.at[u]).start()
        else:
            pltpu.make_async_copy(src.at[:, mid, :, lanes], rows, s_sem.at[u]).start()
            pltpu.make_async_copy(nsrc.at[:, mid, :, lanes], nrows, n_sem.at[u]).start()

    basis = [
        pltpu.make_async_copy(fb.at[pl.ds(0, 5)], fb_buf.at[pl.ds(0, 5)], b_sem.at[0]),
        pltpu.make_async_copy(fb.at[pl.ds(5, 5)], fb_buf.at[pl.ds(5, 5)], b_sem.at[1]),
        pltpu.make_async_copy(mb, mb_buf, b_sem.at[2]),
    ]
    started = set()
    for u in order:
        for kt in range(5):
            start_copies(u, kt, False)
        grp = BLOCKS[u][0]
        if grp not in started:
            started.add(grp)
            basis[grp].start()

    @pl.when(me < OWNERS)
    def _():
        pltpu.make_async_copy(rh0, c_raw.at[0], c_sem.at[0]).start()
        pltpu.make_async_copy(rb0, c_raw.at[1], c_sem.at[0]).start()

        @pl.when(me < TWO_TILES)
        def _():
            pltpu.make_async_copy(rh1, c_raw.at[2], c_sem.at[1]).start()
            pltpu.make_async_copy(rb1, c_raw.at[3], c_sem.at[1]).start()

    rows80 = lax.broadcasted_iota(jnp.int32, (40, 128), 0)
    lane = lax.broadcasted_iota(jnp.int32, (40, 128), 1)
    deg = lax.div(lax.rem(rows80, 10), 2) + lane

    gf[...] = jnp.zeros_like(gf)
    done = set()
    for u in order:
        grp, q = BLOCKS[u]
        which = 1 if grp == 2 else 0
        size = MM if grp == 2 else MF
        first = me * 5 if grp == 2 else me * 10 + grp * 5
        d, a = dec[which], amp[which]
        pltpu.make_async_copy(s_buf.at[u], s_buf.at[u], s_sem.at[u]).wait()
        pltpu.make_async_copy(n_buf.at[u], n_buf.at[u], n_sem.at[u]).wait()
        for kt in range(5):
            inside = deg < size - first - (q * 5 + kt) * 128
            inside = jnp.concatenate([inside, inside], axis=0)

            @pl.loop(0, 8)
            def _(j):
                r = pl.ds(pl.multiple_of(kt * 640 + j * 80, 80), 80)
                val = d * s_buf[u, r, :] + a * n_buf.at[u].reshape(3200, 128)[r, :].astype(F32)
                s_buf[u, r, :] = jnp.where(inside, val, 0.0)

            start_copies(u, kt, True)
            for m in range(5):
                for c in range(2):
                    v = s_buf[u, pl.ds(kt * 640 + m * 2 + c, 64, stride=10), :]
                    a_buf[m, pl.ds(c * 64, 64), pl.ds(kt * 128, 128)] = v.astype(BF16)
        if grp not in done:
            done.add(grp)
            basis[grp].wait()
        for m in range(5):
            if grp == 2:
                b = mb_buf[m]
            else:
                b = fb_buf[grp * 5 + m, :, pl.ds(q * 640, 640)]
            out = lax.dot_general(b, a_buf[m], NT, preferred_element_type=F32)
            if grp < 2 and q == 0:
                acc[m] = out
            else:
                if grp < 2:
                    out = out + acc[m]
                gf[pl.ds(grp * 5 + m, 128, stride=16), :] = out.astype(BF16).astype(F32)

    @pl.when(me < OWNERS)
    def _():
        pltpu.make_async_copy(c_raw.at[pl.ds(0, 2)], c_raw.at[pl.ds(0, 2)], c_sem.at[0]).wait()

        @pl.when(me < TWO_TILES)
        def _():
            pltpu.make_async_copy(c_raw.at[pl.ds(2, 2)], c_raw.at[pl.ds(2, 2)], c_sem.at[1]).wait()

        def add(base, first_time):
            hf[...] = c_raw[base].reshape(1024, 128).astype(F32)
            bf[...] = c_raw[base + 1].reshape(1024, 128).astype(F32)
            for m in range(5):
                h = hf[pl.ds(m, 128, stride=8), :].astype(BF16)
                b = bf[pl.ds(m, 128, stride=8), :].astype(BF16)
                out = lax.dot_general(b, h, NT, preferred_element_type=F32)
                acc[m] = out if first_time else acc[m] + out

        add(0, True)

        @pl.when(me < TWO_TILES)
        def _():
            add(2, False)

        for m in range(5):
            r = pl.ds(10 + m, 128, stride=16)
            gf[r, :] = gf[r, :] + acc[m].astype(BF16).astype(F32)

    g[...] = gf[...].astype(BF16).reshape(128, 16, 128)
    for u in range(5):
        pltpu.make_async_copy(s_buf.at[u], s_buf.at[u], o_sem.at[u]).wait()


def spectral_call(fs, fn, ms, mn, fb, mb, rh0, rh1, rb0, rb1, dec, amp):
    s = jax.ShapeDtypeStruct
    dma = pltpu.SemaphoreType.DMA
    return pl.pallas_call(
        spectral_kernel,
        name="spectral",
        out_shape=(s((NE, 10, 2, MF), F32), s((NE, 5, 2, MM), F32), s((ND, 16, 128), BF16)),
        in_specs=[HBM] * 6 + [ANY] * 4 + [SMEM] * 2,
        out_specs=(HBM, HBM, VMEM),
        scratch_shapes=[
            pltpu.VMEM((5, 3200, 128), F32),
            pltpu.VMEM((5, 320, 5, 2, 128), BF16),
            pltpu.VMEM((10, 128, MF), BF16),
            pltpu.VMEM((5, 128, MM), BF16),
            pltpu.VMEM((5, 128, 640), BF16),
            pltpu.VMEM((5, 128, 128), F32),
            pltpu.VMEM((2048, 128), F32),
            pltpu.VMEM((4, 128, 8, 128), BF16),
            pltpu.VMEM((1024, 128), F32),
            pltpu.VMEM((1024, 128), F32),
            dma((5,)),
            dma((5,)),
            dma((3,)),
            dma((5,)),
            dma((2,)),
        ],
        compiler_params=pltpu.CompilerParams(vmem_limit_bytes=67_000_000),
        cost_estimate=pl.CostEstimate(flops=10**9, bytes_accessed=25 * 10**6, transcendentals=0),
    )(fs, fn, ms, mn, fb, mb, rh0, rh1, rb0, rb1, dec, amp)


def exchange_kernel(g, out, send, recv, here):
    me = my_place()
    own = pltpu.make_async_copy(g.at[me], out.at[me], here)
    own.start()

    @pl.loop(1, ND)
    def _(i):
        d = lax.rem(me + i, ND)
        pltpu.make_async_remote_copy(
            g.at[d], out.at[me], send, recv, device_id=to_device(d), device_id_type=MESH
        ).start()

    own.wait()
    part = out.at[pl.ds(0, ND - 1)]
    pltpu.make_async_copy(part, part, send).wait()
    pltpu.make_async_copy(part, part, recv).wait()


def exchange_call(g):
    return pl.pallas_call(
        exchange_kernel,
        name="exchange",
        out_shape=jax.ShapeDtypeStruct((ND, 16, 128), BF16),
        in_specs=[HBM],
        out_specs=ANY,
        scratch_shapes=[pltpu.SemaphoreType.DMA(())] * 3,
        compiler_params=pltpu.CompilerParams(has_side_effects=True, vmem_limit_bytes=8 * 2**20),
        cost_estimate=pl.CostEstimate(flops=10**6, bytes_accessed=10**6, transcendentals=0),
    )(g)


def synthesis_kernel(rec, w, tw, pat, rf, x, y, pv, sem):
    rf[...] = rec[...].reshape(2048, 128).astype(F32)
    for i in range(10):
        f = rf[pl.ds(i, 128, stride=16), :]
        med = rf[pl.ds(10 + i % 5 + 16 * (i // 5), 64, stride=32), :]
        f = jnp.concatenate([f[:64] + med, f[64:]], axis=0)
        if i == 0:
            row = lax.broadcasted_iota(jnp.int32, (128, 128), 0)
            f = jnp.where(row == 0, f, 2.0 * f)
        else:
            f = 2.0 * f
        t = f.T.astype(BF16)
        x[pl.ds(i * 64, 64), pl.ds(0, 128)] = t[:64]
        x[pl.ds(i * 64, 64), pl.ds(128, 128)] = t[64:]
    y[...] = jnp.dot(x[...], w[...], preferred_element_type=F32)
    view = pv.reshape(20 * 64, 1, 128)
    for half in range(2):
        for j in range(5):
            col = pl.ds(j * 256 + half * 128, 128)
            parts = [None, None]
            for i in range(10):
                yr = y[pl.ds(i * 64, 64), pl.ds(half * 128, 128)]
                if i == 0:
                    term = yr
                else:
                    yi = y[pl.ds(i * 64, 64), pl.ds(256 + half * 128, 128)]
                    term = tw[pl.ds(i, 1), col] * yr - tw[pl.ds(16 + i, 1), col] * yi
                k = i % 2
                parts[k] = term if parts[k] is None else parts[k] + term
            for k, val in ((0, parts[0] + parts[1]), (5, parts[0] - parts[1])):
                lt = (j + k) * 2 + half
                pv[pl.ds(lt * 64, 64), :] = jnp.tanh(val)
                pltpu.make_async_copy(view.at[pl.ds(lt * 64, 64)], pat.at[:, :, pl.ds(lt * 128, 128)], sem).start()
    pltpu.make_async_copy(pv, pv, sem).wait()


def synthesis_call(rec):
    p = np.arange(128)[:, None]
    ang = 2.0 * math.pi * ((p * np.arange(256)[None, :]) % 256) / 256.0
    c, s = np.cos(ang), np.sin(ang)
    w = jnp.asarray(np.block([[c, s], [-s, c]]), BF16)
    i = np.arange(16)[:, None]
    ang = 2.0 * math.pi * ((i * np.arange(1280)[None, :]) % NLON) / NLON
    tw = jnp.asarray(np.concatenate([np.cos(ang), np.sin(ang)]), F32)
    return pl.pallas_call(
        synthesis_kernel,
        name="synthesis",
        out_shape=jax.ShapeDtypeStruct((NE, 1, NLON), F32),
        in_specs=[VMEM] * 3,
        out_specs=HBM,
        scratch_shapes=[
            pltpu.VMEM((2048, 128), F32),
            pltpu.VMEM((640, 256), BF16),
            pltpu.VMEM((640, 512), F32),
            pltpu.VMEM((1280, 128), F32),
            pltpu.SemaphoreType.DMA(()),
        ],
        compiler_params=pltpu.CompilerParams(vmem_limit_bytes=20 * 2**20),
        cost_estimate=pl.CostEstimate(flops=10**8, bytes_accessed=10**6, transcendentals=0),
    )(rec, w, tw)


def body(fs, fn, ms, mn, cs, cn, decay, amplitude, fb, mb, cb):
    fs, fn, ms, mn = (a.transpose(0, 2, 1, 3) for a in (fs, fn, ms, mn))
    coarse_next, h0, h1, b0, b1 = coarse_call(cs, cn, cb, decay, amplitude)
    rh0, rh1, rb0, rb1 = reshard_call(h0, h1, b0, b1)
    fine_next, medium_next, g = spectral_call(fs, fn, ms, mn, fb, mb, rh0, rh1, rb0, rb1, decay, amplitude)
    rec = exchange_call(g)
    pattern = synthesis_call(rec)
    return (fine_next.transpose(0, 2, 1, 3), medium_next.transpose(0, 2, 1, 3), coarse_next, pattern)


def solution(mesh):
    both = ("scale", "lat")
    return jax.shard_map(
        body,
        mesh=mesh,
        in_specs=(
            P(None, None, both, None),
            P(None, None, both, None),
            P(None, None, both, None),
            P(None, None, both, None),
            P("lat", None, None, None),
            P("lat", None, None, None),
            P(),
            P(),
            P(both, None, None),
            P(both, None, None),
            P(both, None, None),
        ),
        out_specs=(
            P(None, None, both, None),
            P(None, None, both, None),
            P("lat", None, None, None),
            P(None, both, None),
        ),
        check_vma=False,
    )
```

time: 185 us -> 62.4 us (0.34)
  other arithmetic: 114 us -> 0 us
  Pallas kernels: 0 us -> 58.6 us
  matrix products: 22.5 us -> 0 us
  starting transfers between devices: 21.3 us -> 0 us
  between operations: 14.2 us -> 0.67 us
  local copies, waits for them, and re-layouts: 11.8 us -> 2.9 us
    another operation x1 -> x0, other arithmetic: 93.9 us -> none
    pallas_call x0 -> x5, Pallas kernels: none -> 58.6 us  [the longest x1 27.3 us: reshard_call(): pl.pallas_call(reshard_kernel, name='coarse_reshard', out_shape=(s, s, s,...]
    dot_general x4 -> x0, matrix products: 22.5 us -> none  [the longest x1 9.65 us: body(): jnp.einsum('ecmk,rmk->ecmr', lax.all_gather(coarse_half, 'lat', axis=0, t...]
    all_to_all x2 -> x0, starting transfers between devices: 21.3 us -> none  [the longest x1 11.5 us: body(): lax.all_to_all(medium_fourier, ('scale', 'lat'), split_axis=3, concat_axi...]
    convert_element_type x3 -> x0, other arithmetic: 20 us -> none  [the longest x1 11.3 us: body(): fine_next.astype(jnp.bfloat16)]
    slice x2 -> x0, local copies, waits for them, and re-layouts: 2.81 us -> none  [body(): coarse_next = advance(coarse_state, coarse_noise, decay[2], amplitude[2], 0)]
    unnamed x11 -> x6, local copies, waits for them, and re-layouts: 5.29 us -> 2.9 us
    convert_element_type x3 -> x0, local copies, waits for them, and re-layouts: 2.34 us -> none  [the longest x1 1.4 us: body(): fine_fourier = jnp.einsum('ecmk,mrk->ecmr', fine_next.astype(jnp.bfloat16...]
  transfers between devices with their start and end apart: 3 -> 0, of which waited for: 0 -> 0; matrix products, arithmetic and copies ran while one was open for 66% -> 0% of each run, Pallas kernels for 0% -> 0%
where the time goes in v1:
time: 62.4 us; the launch traced here: 62.1 us
  Pallas kernels  58.6 us (94%)
  local copies, waits for them, and re-layouts  2.9 us (5%)
  between operations  0.67 us (1%)
    pallas_call x1, Pallas kernels, reshard_call(): pl.pallas_call(reshard_kernel, name='coarse_reshard', out_shape=(s, s, s,...  27.3 us
    pallas_call x1, Pallas kernels, exchange_call(): pl.pallas_call(exchange_kernel, name='exchange', out_shape=jax.ShapeDtype...  14.7 us
    pallas_call x1, Pallas kernels, spectral_call(): pl.pallas_call(spectral_kernel, name='spectral', out_shape=(s((NE, 10, 2,...  12.7 us
    unnamed x6, local copies, waits for them, and re-layouts  2.9 us
    pallas_call x1, Pallas kernels, coarse_call(): pl.pallas_call(coarse_kernel, name='coarse_advance', out_shape=(s((1, 2,...  1.96 us
    pallas_call x1, Pallas kernels, synthesis_call(): pl.pallas_call(synthesis_kernel, name='synthesis', out_shape=jax.ShapeDty...  1.82 us

profile of v1, /device:TPU:1, one launch (start us, length us, event | category | flops | bytes accessed | tf_op | source)
XLA Modules:
  0.0 62.1 jit_solution(14862698114546140830)
XLA Ops:
  0.6 2.0 %coarse_advance.1 = (f32[1,2,160,160]{3,2,1,0:T(8,128)}, bf16[32,8,128]{2,1,0:T(8,128)(2,1)}, bf16[7,8,128]{2,1,0:T(8,128)(2,1)}, bf16[32,8,128]{2,1,0:T(8,128)(2,1)}, bf16[7,8,128]{2,1,0:T(8,128)(2,1)}) custom-call(f32[1,2,160,160]{3,2,1,0:T(8,128)} %cs.1, bf16[1,2,160,160]{3,2,1,0:T(8,128)(2,1)} %cn.1, bf16[1,160,160]{2,1,0:T(8,128)(2,1)} %cb.1, f32[3]{0:T(128)} %dec.3, ...), custom_call_target="tpu_custom_call" | custom-call | flops 1000000 | bytes 1000000 | tf_op jit(solution)/shard_map/coarse_advance/pallas_call | solution.py:55
  2.6 27.3 %coarse_reshard.1 = (bf16[128,8,128]{2,1,0:T(8,128)(2,1)}, bf16[128,8,128]{2,1,0:T(8,128)(2,1)}, bf16[128,8,128]{2,1,0:T(8,128)(2,1)}, bf16[128,8,128]{2,1,0:T(8,128)(2,1)}) custom-call(bf16[32,8,128]{2,1,0:T(8,128)(2,1)} %get-tuple-element.16.h0, bf16[7,8,128]{2,1,0:T(8,128)(2,1)} %get-tuple-element.17.h1, bf16[32,8,128]{2,1,0:T(8,128)(2,1)} %get-tuple-element.18.b0, ...), custom_call_target="tpu_custom_call" | custom-call | flops 1000000 | bytes 1000000 | tf_op jit(solution)/shard_map/coarse_reshard/pallas_call | solution.py:119
  29.9 12.7 %spectral.1 = (f32[64,10,2,1280]{3,2,1,0:T(2,128)}, f32[64,5,2,640]{3,2,1,0:T(2,128)}, bf16[128,16,128]{2,1,0:T(8,128)(2,1)}) custom-call(f32[64,10,2,1280]{3,2,1,0:T(2,128)} %bitcast.6, bf16[64,10,2,1280]{3,2,1,0:T(2,128)(2,1)} %bitcast.7, f32[64,5,2,640]{3,2,1,0:T(2,128)} %bitcast.8, bf16[64,5,2,640]{3,2,1,0:T(2,128)(2,1)} %bitcast.9, ...), custom_call_target="tpu_custom_call" | custom-call | flops 1000000000 | bytes 25000000 | tf_op jit(solution)/shard_map/spectral/pallas_call | solution.py:264
  42.7 0.0 copy-start
  42.7 1.0 %copy-done = bf16[128,16,128]{2,1,0:T(8,128)(2,1)S(1)} copy-done((bf16[128,16,128]{2,1,0:T(8,128)(2,1)S(1)}, bf16[128,16,128]{2,1,0:T(8,128)(2,1)}, u32[]{:S(2)}) %copy-start) | copy-done | bytes 524312
  43.7 14.7 %exchange.1.rec = bf16[128,16,128]{2,1,0:T(8,128)(2,1)S(1)} custom-call(bf16[128,16,128]{2,1,0:T(8,128)(2,1)S(1)} %copy-done), custom_call_target="tpu_custom_call" | custom-call | flops 1000000 | bytes 1000000 | tf_op jit(solution)/shard_map/exchange/pallas_call | solution.py:311
  58.4 0.0 copy-start.1
  58.4 0.9 %copy-done.1 = bf16[256,512]{1,0:T(8,128)(2,1)S(1)} copy-done((bf16[256,512]{1,0:T(8,128)(2,1)S(1)}, bf16[256,512]{1,0:T(8,128)(2,1)}, u32[]{:S(2)}) %copy-start.1) | copy-done | bytes 262168
  59.4 0.0 copy-start.2
  59.4 0.9 %copy-done.2 = f32[32,1280]{1,0:T(8,128)S(1)} copy-done((f32[32,1280]{1,0:T(8,128)S(1)}, f32[32,1280]{1,0:T(8,128)}, u32[]{:S(2)}) %copy-start.2) | copy-done | bytes 163864
  60.3 1.8 %synthesis.1 = f32[64,1,2560]{2,1,0:T(1,128)} custom-call(bf16[128,16,128]{2,1,0:T(8,128)(2,1)S(1)} %exchange.1.rec, bf16[256,512]{1,0:T(8,128)(2,1)S(1)} %copy-done.1, f32[32,1280]{1,0:T(8,128)S(1)} %copy-done.2), custom_call_target="tpu_custom_call" | custom-call | flops 100000000 | bytes 1000000 | tf_op jit(solution)/shard_map/synthesis/pallas_call | solution.py:367
Async XLA Ops:
  42.7 1.0 %copy-start = (bf16[128,16,128]{2,1,0:T(8,128)(2,1)S(1)}, bf16[128,16,128]{2,1,0:T(8,128)(2,1)}, u32[]{:S(2)}) copy-start(bf16[128,16,128]{2,1,0:T(8,128)(2,1)} %get-tuple-element.27.g) | copy-start | bytes 1572868
  58.4 1.0 %copy-start.1 = (bf16[256,512]{1,0:T(8,128)(2,1)S(1)}, bf16[256,512]{1,0:T(8,128)(2,1)}, u32[]{:S(2)}) copy-start(bf16[256,512]{1,0:T(8,128)(2,1)} %constant.4.clone.w) | copy-start | bytes 786436
  59.4 0.9 %copy-start.2 = (f32[32,1280]{1,0:T(8,128)S(1)}, f32[32,1280]{1,0:T(8,128)}, u32[]{:S(2)}) copy-start(f32[32,1280]{1,0:T(8,128)} %constant.5.clone.tw) | copy-start | bytes 491524

commit v2 on v0

v2 whole, which is shorter than its diff:
```python
import math

import jax
import jax.numpy as jnp
import numpy as np
from jax import lax
from jax.experimental import pallas as pl
from jax.experimental.pallas import tpu as pltpu
from jax.sharding import PartitionSpec as P

MESH = pl.DeviceIdType.MESH
F32, BF16 = jnp.float32, jnp.bfloat16
HBM = pl.BlockSpec(memory_space=pltpu.HBM)
VMEM = pl.BlockSpec(memory_space=pltpu.VMEM)
SMEM = pl.BlockSpec(memory_space=pltpu.SMEM)
MF, MM, MC, NLON, NE, NR = 1280, 640, 160, 2560, 64, 128
ND = 128
NT = (((1,), (1,)), ((), ()))


def my_place():
    return lax.axis_index("scale") * 64 + lax.axis_index("lat")


def to_device(d):
    return (d // 64, d % 64)

BLOCKS = [(0, 0), (0, 1), (2, 0), (1, 0), (1, 1)]
STEP = 37


def send_all(me, src, dst, send, recv, here):
    pltpu.make_async_copy(src.at[me], dst.at[me], here).start()

    @pl.loop(1, ND)
    def _(i):
        d = lax.rem(me + i * STEP, ND)
        pltpu.make_async_remote_copy(
            src.at[d], dst.at[me], send, recv, device_id=to_device(d), device_id_type=MESH
        ).start()


def wait_rows(ref, count, sem):
    part = ref.at[pl.ds(0, count)]
    pltpu.make_async_copy(part, part, sem).wait()


def spectral_kernel(
    fs, fn, ms, mn, fb, mb, cs, cn, cb, dec, amp,
    s_buf, c_next, r1, r2, r3, rx,
    n_buf, n_flat, fb_buf, mb_buf, a_buf, acc, stage, g1, g2, g3, gx,
    cs_buf, cn_buf, cb_buf, pad, c_stage, c_msg, c_got,
    s_sem, n_sem, b_sem, c_sem, send, recv, here,
):
    me = my_place()
    scale = lax.axis_index("scale")

    coarse_in = (
        pltpu.make_async_copy(cs, cs_buf, c_sem.at[0]),
        pltpu.make_async_copy(cn, cn_buf, c_sem.at[1]),
        pltpu.make_async_copy(cb, cb_buf, c_sem.at[2]),
    )
    for copy in coarse_in:
        copy.start()

    basis = [
        pltpu.make_async_copy(fb.at[pl.ds(0, 5)], fb_buf.at[pl.ds(0, 5)], b_sem.at[0]),
        pltpu.make_async_copy(fb.at[pl.ds(5, 5)], fb_buf.at[pl.ds(5, 5)], b_sem.at[1]),
        pltpu.make_async_copy(mb, mb_buf, b_sem.at[2]),
    ]
    started = set()
    for u, (grp, q) in enumerate(BLOCKS):
        for kt in range(5):
            lanes = pl.ds((q * 5 + kt) * 128, 128)
            rows = s_buf.at[u].reshape(5 * 64, 5, 2, 128).at[pl.ds(kt * 64, 64)]
            if grp == 2:
                src, nsrc, mid = ms, mn, slice(None)
            else:
                src, nsrc, mid = fs, fn, pl.ds(grp * 5, 5)
            pltpu.make_async_copy(src.at[:, mid, :, lanes], rows, s_sem.at[u]).start()
            pltpu.make_async_copy(nsrc.at[:, mid, :, lanes], n_buf.at[u, pl.ds(kt * 64, 64)], n_sem.at[u]).start()
        if grp not in started:
            started.add(grp)
            basis[grp].start()

    barrier = pltpu.get_barrier_semaphore()

    @pl.loop(1, ND)
    def _(i):
        d = lax.rem(me + i * STEP, ND)
        pl.semaphore_signal(barrier, inc=1, device_id=to_device(d), device_id_type=MESH)

    for copy in coarse_in:
        copy.wait()
    cdeg = lax.broadcasted_iota(jnp.int32, (MC, MC), 0) + lax.broadcasted_iota(jnp.int32, (MC, MC), 1)
    for c in range(2):
        val = dec[2] * cs_buf[0, c] + amp[2] * cn_buf[0, c].astype(F32)
        c_next[0, c] = jnp.where(cdeg < MC, val, 0.0)
    pad[...] = jnp.zeros_like(pad)
    pad[0, :, pl.ds(0, MC)] = c_next[0, scale]
    pad[1, :, pl.ds(0, MC)] = cb_buf[0].astype(F32)
    for k in range(2):
        c_stage[pl.ds(2 * k, 128, stride=4), :] = pad[k, pl.ds(0, 128), pl.ds(0, 128)]
        extra = jnp.concatenate(
            [pad[k, pl.ds(0, 32), pl.ds(128, 128)], pad[k, pl.ds(128, 32), pl.ds(0, 128)], jnp.zeros((64, 128), F32)], axis=0
        )
        c_stage[pl.ds(2 * k + 1, 128, stride=4), :] = extra
    c_msg.reshape(512, 128)[...] = c_stage[...].astype(BF16)

    pl.semaphore_wait(barrier, ND - 1)
    send_all(me, c_msg, c_got, send.at[3], recv.at[3], here.at[3])

    rows40 = lax.broadcasted_iota(jnp.int32, (40, 128), 0)
    deg = lax.div(lax.rem(rows40, 10), 2) + lax.broadcasted_iota(jnp.int32, (40, 128), 1)

    def advance(u, kt):
        grp, q = BLOCKS[u]
        which = 1 if grp == 2 else 0
        size = MM if grp == 2 else MF
        first = me * 5 if grp == 2 else me * 10 + grp * 5
        d, a = dec[which], amp[which]
        inside = deg < size - first - (q * 5 + kt) * 128
        inside = jnp.concatenate([inside, inside], axis=0)

        @pl.loop(0, 8)
        def _(j):
            r = pl.ds(pl.multiple_of(kt * 640 + j * 80, 80), 80)
            n_flat[...] = n_buf.at[u].reshape(3200, 128)[r, :]
            val = d * s_buf[u, r, :] + a * n_flat[...].astype(F32)
            s_buf[u, r, :] = jnp.where(inside, val, 0.0)

        for m in range(5):
            for c in range(2):
                v = s_buf[u, pl.ds(kt * 640 + m * 2 + c, 64, stride=10), :]
                a_buf[m, pl.ds(c * 64, 64), pl.ds(kt * 128, 128)] = v.astype(BF16)

    def legendre(u, put):
        grp, q = BLOCKS[u]
        for m in range(5):
            b = mb_buf[m] if grp == 2 else fb_buf[grp * 5 + m, :, pl.ds(q * 640, 640)]
            out = lax.dot_general(b, a_buf[m], NT, preferred_element_type=F32)
            if grp < 2 and q == 0:
                acc[m] = out
            else:
                put(m, out + acc[m] if grp < 2 else out)

    def begin(u):
        pltpu.make_async_copy(s_buf.at[u], s_buf.at[u], s_sem.at[u]).wait()
        pltpu.make_async_copy(n_buf.at[u], n_buf.at[u], n_sem.at[u]).wait()

    def block(u, put, after_first=None):
        begin(u)
        for kt in range(5):
            advance(u, kt)
            if kt == 0 and after_first is not None:
                after_first()
        if BLOCKS[u][1] == 0:
            basis[BLOCKS[u][0]].wait()
        legendre(u, put)

    def put_first(m, out):
        if m < 4:
            stage[pl.ds(m, 128, stride=4), :] = out
        else:
            acc[0] = out

    block(0, None)
    block(1, put_first)
    g1.reshape(512, 128)[...] = stage[pl.ds(0, 512), :].astype(BF16)
    stage[pl.ds(0, 128, stride=6), :] = acc[0]

    def put_medium(m, out):
        stage[pl.ds(1 + m, 128, stride=6), :] = out

    block(2, put_medium, lambda: send_all(me, g1, r1, send.at[0], recv.at[0], here.at[0]))
    g2.reshape(768, 128)[...] = stage[...].astype(BF16)
    block(3, None, lambda: send_all(me, g2, r2, send.at[1], recv.at[1], here.at[1]))

    wait_rows(c_got, ND - 1, recv.at[3])
    pltpu.make_async_copy(c_got.at[me], c_got.at[me], here.at[3]).wait()
    c_stage[...] = c_got.reshape(512, 128)[...].astype(F32)
    part = [c_stage[pl.ds(k, 128, stride=4), :].astype(BF16) for k in range(4)]
    main = lax.dot_general(part[2], part[0], NT, preferred_element_type=F32)
    extra = lax.dot_general(part[3], part[1], NT, preferred_element_type=F32)
    stage[pl.ds(5, 128, stride=6), :] = main + jnp.where(me < 32, extra, 0.0)
    c_stage[pl.ds(0, 128, stride=2), :] = extra
    c_stage[pl.ds(1, 128, stride=2), :] = jnp.zeros((128, 128), F32)
    gx.reshape(256, 128)[...] = c_stage[pl.ds(0, 256), :].astype(BF16)
    wide = jnp.logical_and(me >= 32, me < 64)
    slot = lax.rem(me, 32)

    def send_extra():
        @pl.when(wide)
        def _():
            pltpu.make_async_copy(gx.at[me], rx.at[slot], here.at[4]).start()

            @pl.loop(1, ND)
            def _(i):
                d = lax.rem(me + i * STEP, ND)
                pltpu.make_async_remote_copy(
                    gx.at[d], rx.at[slot], send.at[4], recv.at[4], device_id=to_device(d), device_id_type=MESH
                ).start()

    def put_last(m, out):
        stage[pl.ds(m, 128, stride=6), :] = out

    block(4, put_last, send_extra)
    g3.reshape(768, 128)[...] = stage[...].astype(BF16)
    send_all(me, g3, r3, send.at[2], recv.at[2], here.at[2])

    wait_rows(c_got, ND - 1, send.at[3])

    @pl.when(wide)
    def _():
        pltpu.make_async_copy(gx.at[0], rx.at[0], here.at[4]).wait()
        wait_rows(gx, ND - 1, send.at[4])
        wait_rows(rx, 31, recv.at[4])

    @pl.when(jnp.logical_not(wide))
    def _():
        wait_rows(rx, 32, recv.at[4])

    for k, r in enumerate((r1, r2, r3)):
        pltpu.make_async_copy(r.at[0], r.at[0], here.at[k]).wait()
        wait_rows(r, ND - 1, send.at[k])
        wait_rows(r, ND - 1, recv.at[k])


def spectral_call(fs, fn, ms, mn, fb, mb, cs, cn, cb, dec, amp):
    dma = pltpu.SemaphoreType.DMA
    v = pltpu.VMEM
    return pl.pallas_call(
        spectral_kernel,
        name="spectral",
        out_shape=(
            v((5, 3200, 128), F32),
            v((1, 2, MC, MC), F32),
            v((ND, 2, 2, 128), BF16),
            v((ND, 3, 2, 128), BF16),
            v((ND, 3, 2, 128), BF16),
            v((32, 2, 128), BF16),
        ),
        in_specs=[HBM] * 9 + [SMEM] * 2,
        out_specs=(VMEM,) * 6,
        scratch_shapes=[
            v((5, 320, 5, 2, 128), BF16),
            v((80, 128), BF16),
            v((10, 128, MF), BF16),
            v((5, 128, MM), BF16),
            v((5, 128, 640), BF16),
            v((5, 128, 128), F32),
            v((768, 128), F32),
            v((ND, 2, 2, 128), BF16),
            v((ND, 3, 2, 128), BF16),
            v((ND, 3, 2, 128), BF16),
            v((ND, 2, 128), BF16),
            v((1, 2, MC, MC), F32),
            v((1, 2, MC, MC), BF16),
            v((1, MC, MC), BF16),
            v((2, MC, 256), F32),
            v((512, 128), F32),
            v((ND, 4, 128), BF16),
            v((ND, 4, 128), BF16),
            dma((5,)),
            dma((5,)),
            dma((3,)),
            dma((3,)),
            dma((5,)),
            dma((5,)),
            dma((5,)),
        ],
        compiler_params=pltpu.CompilerParams(has_side_effects=True, collective_id=0, vmem_limit_bytes=30 * 2**20),
        cost_estimate=pl.CostEstimate(flops=10**9, bytes_accessed=25 * 10**6, transcendentals=0),
    )(fs, fn, ms, mn, fb, mb, cs, cn, cb, dec, amp)


def synthesis_kernel(s_buf, c_next, r1, r2, r3, rx, w, tw, fo, mo, co, pat, f1, f2, f3, cf, x, y, pv, o_sem, c_sem, p_sem):
    for u, (grp, q) in enumerate(BLOCKS):
        for kt in range(5):
            rows = s_buf.at[u].reshape(5 * 64, 5, 2, 128).at[pl.ds(kt * 64, 64)]
            dst, mid = (mo, slice(None)) if grp == 2 else (fo, pl.ds(grp * 5, 5))
            pltpu.make_async_copy(rows, dst.at[:, mid, :, pl.ds((q * 5 + kt) * 128, 128)], o_sem).start()
    coarse_out = pltpu.make_async_copy(c_next, co, c_sem)
    coarse_out.start()

    f1[...] = r1.reshape(512, 128)[...].astype(F32)
    f2[...] = r2.reshape(768, 128)[...].astype(F32)
    f3[...] = r3.reshape(768, 128)[...].astype(F32)
    cf[pl.ds(0, 128), :] = f3[pl.ds(5, 128, stride=6), :]
    y[pl.ds(0, 64), pl.ds(0, 128)] = rx.reshape(64, 128)[...].astype(F32)
    cf[pl.ds(128, 32), :] = y[pl.ds(0, 64), pl.ds(0, 128)].reshape(32, 2, 128)[:, 0, :]
    for i in range(10):
        if i < 4:
            f = f1[pl.ds(i, 128, stride=4), :]
        elif i == 4:
            f = f2[pl.ds(0, 128, stride=6), :]
        else:
            f = f3[pl.ds(i - 5, 128, stride=6), :]
        med = f2[pl.ds(1 + i % 5 + 6 * (i // 5), 64, stride=12), :]
        coarse = cf[pl.ds(i, 16, stride=10), :]
        f = jnp.concatenate([f[:16] + (med[:16] + coarse), f[16:64] + med[16:], f[64:]], axis=0)
        if i == 0:
            row = lax.broadcasted_iota(jnp.int32, (128, 128), 0)
            f = jnp.where(row == 0, f, 2.0 * f)
        else:
            f = 2.0 * f
        t = f.T.astype(BF16)
        x[pl.ds(i * 64, 64), pl.ds(0, 128)] = t[:64]
        x[pl.ds(i * 64, 64), pl.ds(128, 128)] = t[64:]
    y[...] = jnp.dot(x[...], w[...], preferred_element_type=F32)
    view = pv.reshape(20 * 64, 1, 128)
    for half in range(2):
        for j in range(5):
            col = pl.ds(j * 256 + half * 128, 128)
            parts = [None, None]
            for i in range(10):
                yr = y[pl.ds(i * 64, 64), pl.ds(half * 128, 128)]
                if i == 0:
                    term = yr
                else:
                    yi = y[pl.ds(i * 64, 64), pl.ds(256 + half * 128, 128)]
                    term = tw[pl.ds(i, 1), col] * yr - tw[pl.ds(16 + i, 1), col] * yi
                k = i % 2
                parts[k] = term if parts[k] is None else parts[k] + term
            for k, val in ((0, parts[0] + parts[1]), (5, parts[0] - parts[1])):
                lt = (j + k) * 2 + half
                pv[pl.ds(lt * 64, 64), :] = jnp.tanh(val)
                pltpu.make_async_copy(view.at[pl.ds(lt * 64, 64)], pat.at[:, :, pl.ds(lt * 128, 128)], p_sem).start()
    pltpu.make_async_copy(s_buf, s_buf, o_sem).wait()
    coarse_out.wait()
    pltpu.make_async_copy(pv, pv, p_sem).wait()


def synthesis_call(*parts):
    p = np.arange(128)[:, None]
    ang = 2.0 * math.pi * ((p * np.arange(256)[None, :]) % 256) / 256.0
    c, s = np.cos(ang), np.sin(ang)
    w = jnp.asarray(np.block([[c, s], [-s, c]]), BF16)
    i = np.arange(16)[:, None]
    ang = 2.0 * math.pi * ((i * np.arange(1280)[None, :]) % NLON) / NLON
    tw = jnp.asarray(np.concatenate([np.cos(ang), np.sin(ang)]), F32)
    s = jax.ShapeDtypeStruct
    v = pltpu.VMEM
    return pl.pallas_call(
        synthesis_kernel,
        name="synthesis",
        out_shape=(
            s((NE, 10, 2, MF), F32),
            s((NE, 5, 2, MM), F32),
            s((1, 2, MC, MC), F32),
            s((NE, 1, NLON), F32),
        ),
        in_specs=[VMEM] * 8,
        out_specs=(HBM,) * 4,
        scratch_shapes=[
            v((512, 128), F32),
            v((768, 128), F32),
            v((768, 128), F32),
            v((160, 128), F32),
            v((640, 256), BF16),
            v((640, 512), F32),
            v((1280, 128), F32),
            pltpu.SemaphoreType.DMA(()),
            pltpu.SemaphoreType.DMA(()),
            pltpu.SemaphoreType.DMA(()),
        ],
        compiler_params=pltpu.CompilerParams(vmem_limit_bytes=20 * 2**20),
        cost_estimate=pl.CostEstimate(flops=10**8, bytes_accessed=10**7, transcendentals=0),
    )(*parts, w, tw)


def body(fs, fn, ms, mn, cs, cn, decay, amplitude, fb, mb, cb):
    fs, fn, ms, mn = (a.transpose(0, 2, 1, 3) for a in (fs, fn, ms, mn))
    big = [pltpu.with_memory_space_constraint(a, pltpu.HBM) for a in (fs, fn, ms, mn, fb, mb, cs, cn, cb)]
    parts = spectral_call(*big, decay, amplitude)
    fine_next, medium_next, coarse_next, pattern = synthesis_call(*parts)
    return (fine_next.transpose(0, 2, 1, 3), medium_next.transpose(0, 2, 1, 3), coarse_next, pattern)


def solution(mesh):
    both = ("scale", "lat")
    return jax.shard_map(
        body,
        mesh=mesh,
        in_specs=(
            P(None, None, both, None),
            P(None, None, both, None),
            P(None, None, both, None),
            P(None, None, both, None),
            P("lat", None, None, None),
            P("lat", None, None, None),
            P(),
            P(),
            P(both, None, None),
            P(both, None, None),
            P(both, None, None),
        ),
        out_specs=(
            P(None, None, both, None),
            P(None, None, both, None),
            P("lat", None, None, None),
            P(None, both, None),
        ),
        check_vma=False,
    )
```

time: 185 us -> 45 us (0.24)
  other arithmetic: 114 us -> 0 us
  Pallas kernels: 0 us -> 42.9 us
  matrix products: 22.5 us -> 0 us
  starting transfers between devices: 21.3 us -> 0 us
  between operations: 14.2 us -> 0.67 us
  local copies, waits for them, and re-layouts: 11.8 us -> 1.31 us
    another operation x1 -> x0, other arithmetic: 93.9 us -> none
    pallas_call x0 -> x2, Pallas kernels: none -> 42.9 us  [the longest x1 39.3 us: spectral_call(): pl.pallas_call(spectral_kernel, name='spectral', out_shape=(v((5, 3200, 1...]
    dot_general x4 -> x0, matrix products: 22.5 us -> none  [the longest x1 9.65 us: body(): jnp.einsum('ecmk,rmk->ecmr', lax.all_gather(coarse_half, 'lat', axis=0, t...]
    all_to_all x2 -> x0, starting transfers between devices: 21.3 us -> none  [the longest x1 11.5 us: body(): lax.all_to_all(medium_fourier, ('scale', 'lat'), split_axis=3, concat_axi...]
    convert_element_type x3 -> x0, other arithmetic: 20 us -> none  [the longest x1 11.3 us: body(): fine_next.astype(jnp.bfloat16)]
    unnamed x11 -> x8, local copies, waits for them, and re-layouts: 5.29 us -> 1.31 us
    slice x2 -> x0, local copies, waits for them, and re-layouts: 2.81 us -> none  [body(): coarse_next = advance(coarse_state, coarse_noise, decay[2], amplitude[2], 0)]
    convert_element_type x3 -> x0, local copies, waits for them, and re-layouts: 2.34 us -> none  [the longest x1 1.4 us: body(): fine_fourier = jnp.einsum('ecmk,mrk->ecmr', fine_next.astype(jnp.bfloat16...]
  transfers between devices with their start and end apart: 3 -> 0, of which waited for: 0 -> 0; matrix products, arithmetic and copies ran while one was open for 66% -> 0% of each run, Pallas kernels for 0% -> 0%
where the time goes in v2:
time: 45 us; the launch traced here: 44.8 us
  Pallas kernels  42.9 us (95%)
  local copies, waits for them, and re-layouts  1.31 us (3%)
  between operations  0.67 us (1%)
    pallas_call x1, Pallas kernels, spectral_call(): pl.pallas_call(spectral_kernel, name='spectral', out_shape=(v((5, 3200, 1...  39.3 us
    pallas_call x1, Pallas kernels, synthesis_call(): pl.pallas_call(synthesis_kernel, name='synthesis', out_shape=(s((NE, 10,...  3.51 us
    unnamed x8, local copies, waits for them, and re-layouts  1.31 us

profile of v2, /device:TPU:1, one launch (start us, length us, event | category | flops | bytes accessed | tf_op | source)
XLA Modules:
  0.0 44.8 jit_solution(4397916891480717961)
XLA Ops:
  0.6 0.0 copy-start.2
  0.6 0.6 %copy-done.2 = f32[3]{0:T(128)S(1)} copy-done((f32[3]{0:T(128)S(1)}, f32[3]{0:T(128)}, u32[]{:S(2)}) %copy-start.2) | copy-done | bytes 36
  1.3 0.0 copy-start.3
  1.3 0.7 %copy-done.3 = f32[3]{0:T(128)S(1)} copy-done((f32[3]{0:T(128)S(1)}, f32[3]{0:T(128)}, u32[]{:S(2)}) %copy-start.3) | copy-done | bytes 36
  1.9 0.0 copy-start
  1.9 0.0 copy-start.1
  2.0 39.3 %spectral.1 = (f32[5,3200,128]{2,1,0:T(8,128)S(1)}, f32[1,2,160,160]{3,2,1,0:T(8,128)S(1)}, bf16[128,2,2,128]{3,2,1,0:T(2,128)(2,1)S(1)}, bf16[128,3,2,128]{3,2,...) custom-call(f32[64,10,2,1280]{3,2,1,0:T(2,128)} %bitcast.6, ...), custom_call_target="tpu_custom_call" | custom-call | flops 1000000000 | bytes 25000000 | tf_op jit(solution)/shard_map/spectral/pallas_call | solution.py:232
  41.3 0.0 copy-done
  41.3 0.0 copy-done.1
  41.3 3.5 %synthesis.1 = (f32[64,10,2,1280]{3,2,1,0:T(2,128)}, f32[64,5,2,640]{3,2,1,0:T(2,128)}, f32[1,2,160,160]{3,2,1,0:T(8,128)}, f32[64,1,2560]{2,1,0:T(1,128)}) custom-call(f32[5,3200,128]{2,1,0:T(8,128)S(1)} %get-tuple-element.14.s_buf, f32[1,2,160,160]{3,2,1,0:T(8,128)S(1)} %get-tuple-element.15.c_next, bf16[128,2,2,128]{3,2,1,0:T(2,128)(2,1)S(1)} %get-tuple-element.16.r1, ...), custom_call_target="tpu_custom_call" | custom-call | flops 100000000 | bytes 10000000 | tf_op jit(solution)/shard_map/synthesis/pallas_call | solution.py:344
Async XLA Ops:
  0.6 0.7 %copy-start.2 = (f32[3]{0:T(128)S(1)}, f32[3]{0:T(128)}, u32[]{:S(2)}) copy-start(f32[3]{0:T(128)} %dec.1) | copy-start | bytes 40
  1.3 0.7 %copy-start.3 = (f32[3]{0:T(128)S(1)}, f32[3]{0:T(128)}, u32[]{:S(2)}) copy-start(f32[3]{0:T(128)} %amp.1) | copy-start | bytes 40
  1.9 39.4 %copy-start = (bf16[256,512]{1,0:T(8,128)(2,1)S(1)}, bf16[256,512]{1,0:T(8,128)(2,1)}, u32[]{:S(2)}) copy-start(bf16[256,512]{1,0:T(8,128)(2,1)} %constant.4.clone.w) | copy-start | bytes 786436
  1.9 39.4 %copy-start.1 = (f32[32,1280]{1,0:T(8,128)S(1)}, f32[32,1280]{1,0:T(8,128)}, u32[]{:S(2)}) copy-start(f32[32,1280]{1,0:T(8,128)} %constant.5.clone.tw) | copy-start | bytes 491524

commit v3 on v2

--- a/solution.py
+++ b/solution.py
@@ -8,7 +8,7 @@
 from jax.experimental.pallas import tpu as pltpu
 from jax.sharding import PartitionSpec as P
 
-MESH = pl.DeviceIdType.MESH
+LOGICAL = pl.DeviceIdType.LOGICAL
 F32, BF16 = jnp.float32, jnp.bfloat16
 HBM = pl.BlockSpec(memory_space=pltpu.HBM)
 VMEM = pl.BlockSpec(memory_space=pltpu.VMEM)
@@ -22,22 +22,29 @@
     return lax.axis_index("scale") * 64 + lax.axis_index("lat")
 
 
-def to_device(d):
-    return (d // 64, d % 64)
-
 BLOCKS = [(0, 0), (0, 1), (2, 0), (1, 0), (1, 1)]
-STEP = 37
+
+
+def others(me, act):
+    @pl.loop(0, 9)
+    def _(t):
+        for k in range(14):
+            d = me + (1 + 9 * k) + t
+            act(jnp.where(d >= ND, d - ND, d))
+
+    d = me + (ND - 1)
+    act(jnp.where(d >= ND, d - ND, d))
 
 
 def send_all(me, src, dst, send, recv, here):
     pltpu.make_async_copy(src.at[me], dst.at[me], here).start()
 
-    @pl.loop(1, ND)
-    def _(i):
-        d = lax.rem(me + i * STEP, ND)
+    def one(d):
         pltpu.make_async_remote_copy(
-            src.at[d], dst.at[me], send, recv, device_id=to_device(d), device_id_type=MESH
+            src.at[d], dst.at[me], send, recv, device_id=d, device_id_type=LOGICAL
         ).start()
+
+    others(me, one)
 
 
 def wait_rows(ref, count, sem):
@@ -47,8 +54,8 @@
 
 def spectral_kernel(
     fs, fn, ms, mn, fb, mb, cs, cn, cb, dec, amp,
-    s_buf, c_next, r1, r2, r3, rx,
-    n_buf, n_flat, fb_buf, mb_buf, a_buf, acc, stage, g1, g2, g3, gx,
+    s_buf, c_next, r1, r2, rx,
+    n_buf, n_flat, fb_buf, mb_buf, a_buf, acc, stage, g1, g2, gx,
     cs_buf, cn_buf, cb_buf, pad, c_stage, c_msg, c_got,
     s_sem, n_sem, b_sem, c_sem, send, recv, here,
 ):
@@ -85,10 +92,7 @@
 
     barrier = pltpu.get_barrier_semaphore()
 
-    @pl.loop(1, ND)
-    def _(i):
-        d = lax.rem(me + i * STEP, ND)
-        pl.semaphore_signal(barrier, inc=1, device_id=to_device(d), device_id_type=MESH)
+    others(me, lambda d: pl.semaphore_signal(barrier, inc=1, device_id=d, device_id_type=LOGICAL))
 
     for copy in coarse_in:
         copy.wait()
@@ -107,9 +111,6 @@
         c_stage[pl.ds(2 * k + 1, 128, stride=4), :] = extra
     c_msg.reshape(512, 128)[...] = c_stage[...].astype(BF16)
 
-    pl.semaphore_wait(barrier, ND - 1)
-    send_all(me, c_msg, c_got, send.at[3], recv.at[3], here.at[3])
-
     rows40 = lax.broadcasted_iota(jnp.int32, (40, 128), 0)
     deg = lax.div(lax.rem(rows40, 10), 2) + lax.broadcasted_iota(jnp.int32, (40, 128), 1)
 
@@ -159,22 +160,18 @@
         legendre(u, put)
 
     def put_first(m, out):
-        if m < 4:
-            stage[pl.ds(m, 128, stride=4), :] = out
-        else:
-            acc[0] = out
+        stage[pl.ds(m, 128, stride=10), :] = out
+
+    def put_medium(m, out):
+        stage[pl.ds(5 + m, 128, stride=10), :] = out
 
     block(0, None)
+    pl.semaphore_wait(barrier, ND - 1)
+    send_all(me, c_msg, c_got, send.at[3], recv.at[3], here.at[3])
     block(1, put_first)
-    g1.reshape(512, 128)[...] = stage[pl.ds(0, 512), :].astype(BF16)
-    stage[pl.ds(0, 128, stride=6), :] = acc[0]
-
-    def put_medium(m, out):
-        stage[pl.ds(1 + m, 128, stride=6), :] = out
-
-    block(2, put_medium, lambda: send_all(me, g1, r1, send.at[0], recv.at[0], here.at[0]))
-    g2.reshape(768, 128)[...] = stage[...].astype(BF16)
-    block(3, None, lambda: send_all(me, g2, r2, send.at[1], recv.at[1], here.at[1]))
+    block(2, put_medium)
+    g1.reshape(1280, 128)[...] = stage[...].astype(BF16)
+    block(3, None, lambda: send_all(me, g1, r1, send.at[0], recv.at[0], here.at[0]))
 
     wait_rows(c_got, ND - 1, recv.at[3])
     pltpu.make_async_copy(c_got.at[me], c_got.at[me], here.at[3]).wait()
@@ -194,19 +191,19 @@
         def _():
             pltpu.make_async_copy(gx.at[me], rx.at[slot], here.at[4]).start()
 
-            @pl.loop(1, ND)
-            def _(i):
-                d = lax.rem(me + i * STEP, ND)
+            def one(d):
                 pltpu.make_async_remote_copy(
-                    gx.at[d], rx.at[slot], send.at[4], recv.at[4], device_id=to_device(d), device_id_type=MESH
+                    gx.at[d], rx.at[slot], send.at[4], recv.at[4], device_id=d, device_id_type=LOGICAL
                 ).start()
+
+            others(me, one)
 
     def put_last(m, out):
         stage[pl.ds(m, 128, stride=6), :] = out
 
     block(4, put_last, send_extra)
-    g3.reshape(768, 128)[...] = stage[...].astype(BF16)
-    send_all(me, g3, r3, send.at[2], recv.at[2], here.at[2])
+    g2.reshape(768, 128)[...] = stage[pl.ds(0, 768), :].astype(BF16)
+    send_all(me, g2, r2, send.at[1], recv.at[1], here.at[1])
 
     wait_rows(c_got, ND - 1, send.at[3])
 
@@ -220,7 +217,7 @@
     def _():
         wait_rows(rx, 32, recv.at[4])
 
-    for k, r in enumerate((r1, r2, r3)):
+    for k, r in enumerate((r1, r2)):
         pltpu.make_async_copy(r.at[0], r.at[0], here.at[k]).wait()
         wait_rows(r, ND - 1, send.at[k])
         wait_rows(r, ND - 1, recv.at[k])
@@ -235,13 +232,12 @@
         out_shape=(
             v((5, 3200, 128), F32),
             v((1, 2, MC, MC), F32),
-            v((ND, 2, 2, 128), BF16),
-            v((ND, 3, 2, 128), BF16),
+            v((ND, 5, 2, 128), BF16),
             v((ND, 3, 2, 128), BF16),
             v((32, 2, 128), BF16),
         ),
         in_specs=[HBM] * 9 + [SMEM] * 2,
-        out_specs=(VMEM,) * 6,
+        out_specs=(VMEM,) * 5,
         scratch_shapes=[
             v((5, 320, 5, 2, 128), BF16),
             v((80, 128), BF16),
@@ -249,9 +245,8 @@
             v((5, 128, MM), BF16),
             v((5, 128, 640), BF16),
             v((5, 128, 128), F32),
-            v((768, 128), F32),
-            v((ND, 2, 2, 128), BF16),
-            v((ND, 3, 2, 128), BF16),
+            v((1280, 128), F32),
+            v((ND, 5, 2, 128), BF16),
             v((ND, 3, 2, 128), BF16),
             v((ND, 2, 128), BF16),
             v((1, 2, MC, MC), F32),
@@ -274,7 +269,7 @@
     )(fs, fn, ms, mn, fb, mb, cs, cn, cb, dec, amp)
 
 
-def synthesis_kernel(s_buf, c_next, r1, r2, r3, rx, w, tw, fo, mo, co, pat, f1, f2, f3, cf, x, y, pv, o_sem, c_sem, p_sem):
+def synthesis_kernel(s_buf, c_next, r1, r2, rx, w, tw, fo, mo, co, pat, f1, f2, cf, x, y, pv, o_sem, c_sem, p_sem):
     for u, (grp, q) in enumerate(BLOCKS):
         for kt in range(5):
             rows = s_buf.at[u].reshape(5 * 64, 5, 2, 128).at[pl.ds(kt * 64, 64)]
@@ -283,20 +278,17 @@
     coarse_out = pltpu.make_async_copy(c_next, co, c_sem)
     coarse_out.start()
 
-    f1[...] = r1.reshape(512, 128)[...].astype(F32)
+    f1[...] = r1.reshape(1280, 128)[...].astype(F32)
     f2[...] = r2.reshape(768, 128)[...].astype(F32)
-    f3[...] = r3.reshape(768, 128)[...].astype(F32)
-    cf[pl.ds(0, 128), :] = f3[pl.ds(5, 128, stride=6), :]
+    cf[pl.ds(0, 128), :] = f2[pl.ds(5, 128, stride=6), :]
     y[pl.ds(0, 64), pl.ds(0, 128)] = rx.reshape(64, 128)[...].astype(F32)
     cf[pl.ds(128, 32), :] = y[pl.ds(0, 64), pl.ds(0, 128)].reshape(32, 2, 128)[:, 0, :]
     for i in range(10):
-        if i < 4:
-            f = f1[pl.ds(i, 128, stride=4), :]
-        elif i == 4:
-            f = f2[pl.ds(0, 128, stride=6), :]
+        if i < 5:
+            f = f1[pl.ds(i, 128, stride=10), :]
         else:
-            f = f3[pl.ds(i - 5, 128, stride=6), :]
-        med = f2[pl.ds(1 + i % 5 + 6 * (i // 5), 64, stride=12), :]
+            f = f2[pl.ds(i - 5, 128, stride=6), :]
+        med = f1[pl.ds(5 + i % 5 + 10 * (i // 5), 64, stride=20), :]
         coarse = cf[pl.ds(i, 16, stride=10), :]
         f = jnp.concatenate([f[:16] + (med[:16] + coarse), f[16:64] + med[16:], f[64:]], axis=0)
         if i == 0:
@@ -350,11 +342,10 @@
             s((1, 2, MC, MC), F32),
             s((NE, 1, NLON), F32),
         ),
-        in_specs=[VMEM] * 8,
+        in_specs=[VMEM] * 7,
         out_specs=(HBM,) * 4,
         scratch_shapes=[
-            v((512, 128), F32),
-            v((768, 128), F32),
+            v((1280, 128), F32),
             v((768, 128), F32),
             v((160, 128), F32),
             v((640, 256), BF16),

time: 45 us -> 32.6 us (0.72)
  Pallas kernels: 42.9 us -> 30.5 us
    pallas_call x1, Pallas kernels: 39.3 us -> 27 us  [spectral_call(): pl.pallas_call(spectral_kernel, name='spectral', out_shape=(v((5, 3200, 1...]
where the time goes in v3:
time: 32.6 us; the launch traced here: 32.4 us
  Pallas kernels  30.5 us (94%)
  local copies, waits for them, and re-layouts  1.31 us (4%)
  between operations  0.67 us (2%)
    pallas_call x1, Pallas kernels, spectral_call(): pl.pallas_call(spectral_kernel, name='spectral', out_shape=(v((5, 3200, 1...  27 us
    pallas_call x1, Pallas kernels, synthesis_call(): pl.pallas_call(synthesis_kernel, name='synthesis', out_shape=(s((NE, 10,...  3.51 us
    unnamed x8, local copies, waits for them, and re-layouts  1.31 us

profile of v3, /device:TPU:1, one launch (start us, length us, event | category | flops | bytes accessed | tf_op | source)
XLA Modules:
  0.0 32.4 jit_solution(1214018054260513455)
XLA Ops:
  0.6 0.0 copy-start.2
  0.6 0.6 %copy-done.2 = f32[3]{0:T(128)S(1)} copy-done((f32[3]{0:T(128)S(1)}, f32[3]{0:T(128)}, u32[]{:S(2)}) %copy-start.2) | copy-done | bytes 36
  1.3 0.0 copy-start.3
  1.3 0.7 %copy-done.3 = f32[3]{0:T(128)S(1)} copy-done((f32[3]{0:T(128)S(1)}, f32[3]{0:T(128)}, u32[]{:S(2)}) %copy-start.3) | copy-done | bytes 36
  1.9 0.0 copy-start
  1.9 0.0 copy-start.1
  2.0 27.0 %spectral.1 = (f32[5,3200,128]{2,1,0:T(8,128)S(1)}, f32[1,2,160,160]{3,2,1,0:T(8,128)S(1)}, bf16[128,5,2,128]{3,2,1,0:T(2,128)(2,1)S(1)}, bf16[128,3,2,128]{3,2,1,0:T(2,128)(2,1)S(1)}, bf16[32,2,128]{2,1,0:T(2,128)(2,1)S(1)}) custom-call(f32[64,10,2,1280]{3,2,1,0:T(2,128)} %bitcast.6, bf16[64,10,2,1280]{3,2,1,0:T(2,128)(2,1)} %bitcast.7, ...), custom_call_target="tpu_custom_call" | custom-call | flops 1000000000 | bytes 25000000 | tf_op jit(solution)/shard_map/spectral/pallas_call | solution.py:229
  28.9 0.0 copy-done
  28.9 0.0 copy-done.1
  28.9 3.5 %synthesis.1 = (f32[64,10,2,1280]{3,2,1,0:T(2,128)}, f32[64,5,2,640]{3,2,1,0:T(2,128)}, f32[1,2,160,160]{3,2,1,0:T(8,128)}, f32[64,1,2560]{2,1,0:T(1,128)}) custom-call(f32[5,3200,128]{2,1,0:T(8,128)S(1)} %get-tuple-element.13.s_buf, f32[1,2,160,160]{3,2,1,0:T(8,128)S(1)} %get-tuple-element.14.c_next, bf16[128,5,2,128]{3,2,1,0:T(2,128)(2,1)S(1)} %get-tuple-element.15.r1, ...), custom_call_target="tpu_custom_call" | custom-call | flops 100000000 | bytes 10000000 | tf_op jit(solution)/shard_map/synthesis/pallas_call | solution.py:336
Async XLA Ops:
  0.6 0.7 %copy-start.2 = (f32[3]{0:T(128)S(1)}, f32[3]{0:T(128)}, u32[]{:S(2)}) copy-start(f32[3]{0:T(128)} %dec.1) | copy-start | bytes 40
  1.3 0.7 %copy-start.3 = (f32[3]{0:T(128)S(1)}, f32[3]{0:T(128)}, u32[]{:S(2)}) copy-start(f32[3]{0:T(128)} %amp.1) | copy-start | bytes 40
  1.9 27.0 %copy-start = (bf16[256,512]{1,0:T(8,128)(2,1)S(1)}, bf16[256,512]{1,0:T(8,128)(2,1)}, u32[]{:S(2)}) copy-start(bf16[256,512]{1,0:T(8,128)(2,1)} %constant.4.clone.w) | copy-start | bytes 786436
  1.9 27.0 %copy-start.1 = (f32[32,1280]{1,0:T(8,128)S(1)}, f32[32,1280]{1,0:T(8,128)}, u32[]{:S(2)}) copy-start(f32[32,1280]{1,0:T(8,128)} %constant.5.clone.tw) | copy-start | bytes 491524

commit v4 on v3

--- a/solution.py
+++ b/solution.py
@@ -12,7 +12,6 @@
 F32, BF16 = jnp.float32, jnp.bfloat16
 HBM = pl.BlockSpec(memory_space=pltpu.HBM)
 VMEM = pl.BlockSpec(memory_space=pltpu.VMEM)
-SMEM = pl.BlockSpec(memory_space=pltpu.SMEM)
 MF, MM, MC, NLON, NE, NR = 1280, 640, 160, 2560, 64, 128
 ND = 128
 NT = (((1,), (1,)), ((), ()))
@@ -22,18 +21,27 @@
     return lax.axis_index("scale") * 64 + lax.axis_index("lat")
 
 
-BLOCKS = [(0, 0), (0, 1), (2, 0), (1, 0), (1, 1)]
-
-
-def others(me, act):
-    @pl.loop(0, 9)
+BLOCKS = [(2, 0), (0, 0), (0, 1), (1, 0), (1, 1)]
+
+
+def others(act):
+    lat = lax.axis_index("lat")
+    y = lax.axis_index("scale") * 2 + lax.rem(lax.div(lat, 2), 2)
+    x, z, core = lax.div(lat, 16), lax.rem(lax.div(lat, 4), 4), lax.rem(lat, 2)
+    low = []
+    for dy in (2, 1, 3, 0):
+        for dc in (1, 0):
+            yy = lax.rem(y + dy, 4)
+            low.append(lax.div(yy, 2) * 64 + lax.rem(yy, 2) * 2 + lax.rem(core + dc, 2))
+
+    @pl.loop(0, 15)
     def _(t):
-        for k in range(14):
-            d = me + (1 + 9 * k) + t
-            act(jnp.where(d >= ND, d - ND, d))
-
-    d = me + (ND - 1)
-    act(jnp.where(d >= ND, d - ND, d))
+        high = lax.rem(x + 1 + lax.div(t, 4), 4) * 16 + lax.rem(z + 1 + t, 4) * 4
+        for part in low:
+            act(high + part)
+
+    for part in low[:-1]:
+        act(x * 16 + z * 4 + part)
 
 
 def send_all(me, src, dst, send, recv, here):
@@ -44,7 +52,7 @@
             src.at[d], dst.at[me], send, recv, device_id=d, device_id_type=LOGICAL
         ).start()
 
-    others(me, one)
+    others(one)
 
 
 def wait_rows(ref, count, sem):
@@ -53,11 +61,11 @@
 
 
 def spectral_kernel(
-    fs, fn, ms, mn, fb, mb, cs, cn, cb, dec, amp,
-    s_buf, c_next, r1, r2, rx,
-    n_buf, n_flat, fb_buf, mb_buf, a_buf, acc, stage, g1, g2, gx,
+    fs, fn, ms, mn, fb, mb, cs, cn, cb, dec_in, amp_in,
+    s_buf, c_next, r1, r2, r3, rc,
+    n_buf, n_flat, fb_buf, mb_buf, a_buf, acc, stage1, stage2, stage3, g1, g2, g3, gc,
     cs_buf, cn_buf, cb_buf, pad, c_stage, c_msg, c_got,
-    s_sem, n_sem, b_sem, c_sem, send, recv, here,
+    dec, amp, s_sem, n_sem, b_sem, c_sem, send, recv, here,
 ):
     me = my_place()
     scale = lax.axis_index("scale")
@@ -66,9 +74,15 @@
         pltpu.make_async_copy(cs, cs_buf, c_sem.at[0]),
         pltpu.make_async_copy(cn, cn_buf, c_sem.at[1]),
         pltpu.make_async_copy(cb, cb_buf, c_sem.at[2]),
+        pltpu.make_async_copy(dec_in, dec, c_sem.at[3]),
+        pltpu.make_async_copy(amp_in, amp, c_sem.at[4]),
     )
     for copy in coarse_in:
         copy.start()
+
+    barrier = pltpu.get_barrier_semaphore()
+
+    others(lambda d: pl.semaphore_signal(barrier, inc=1, device_id=d, device_id_type=LOGICAL))
 
     basis = [
         pltpu.make_async_copy(fb.at[pl.ds(0, 5)], fb_buf.at[pl.ds(0, 5)], b_sem.at[0]),
@@ -90,10 +104,6 @@
             started.add(grp)
             basis[grp].start()
 
-    barrier = pltpu.get_barrier_semaphore()
-
-    others(me, lambda d: pl.semaphore_signal(barrier, inc=1, device_id=d, device_id_type=LOGICAL))
-
     for copy in coarse_in:
         copy.wait()
     cdeg = lax.broadcasted_iota(jnp.int32, (MC, MC), 0) + lax.broadcasted_iota(jnp.int32, (MC, MC), 1)
@@ -122,56 +132,73 @@
         d, a = dec[which], amp[which]
         inside = deg < size - first - (q * 5 + kt) * 128
         inside = jnp.concatenate([inside, inside], axis=0)
-
-        @pl.loop(0, 8)
-        def _(j):
-            r = pl.ds(pl.multiple_of(kt * 640 + j * 80, 80), 80)
-            n_flat[...] = n_buf.at[u].reshape(3200, 128)[r, :]
-            val = d * s_buf[u, r, :] + a * n_flat[...].astype(F32)
+        noise = n_buf.at[u].reshape(3200, 128)
+        for j in range(8):
+            r = pl.ds(kt * 640 + j * 80, 80)
+            n_flat[pl.ds(j * 80, 80), :] = noise[r, :]
+            val = d * s_buf[u, r, :] + a * n_flat[pl.ds(j * 80, 80), :].astype(F32)
             s_buf[u, r, :] = jnp.where(inside, val, 0.0)
-
         for m in range(5):
             for c in range(2):
                 v = s_buf[u, pl.ds(kt * 640 + m * 2 + c, 64, stride=10), :]
-                a_buf[m, pl.ds(c * 64, 64), pl.ds(kt * 128, 128)] = v.astype(BF16)
-
-    def legendre(u, put):
+                a_buf[u % 2, m, pl.ds(c * 64, 64), pl.ds(kt * 128, 128)] = v.astype(BF16)
+
+    def legendre(u, m):
         grp, q = BLOCKS[u]
-        for m in range(5):
-            b = mb_buf[m] if grp == 2 else fb_buf[grp * 5 + m, :, pl.ds(q * 640, 640)]
-            out = lax.dot_general(b, a_buf[m], NT, preferred_element_type=F32)
-            if grp < 2 and q == 0:
-                acc[m] = out
-            else:
-                put(m, out + acc[m] if grp < 2 else out)
-
-    def begin(u):
-        pltpu.make_async_copy(s_buf.at[u], s_buf.at[u], s_sem.at[u]).wait()
-        pltpu.make_async_copy(n_buf.at[u], n_buf.at[u], n_sem.at[u]).wait()
-
-    def block(u, put, after_first=None):
-        begin(u)
-        for kt in range(5):
-            advance(u, kt)
-            if kt == 0 and after_first is not None:
-                after_first()
-        if BLOCKS[u][1] == 0:
-            basis[BLOCKS[u][0]].wait()
-        legendre(u, put)
+        b = mb_buf[m] if grp == 2 else fb_buf[grp * 5 + m, :, pl.ds(q * 640, 640)]
+        out = lax.dot_general(b, a_buf[u % 2, m], NT, preferred_element_type=F32)
+        if grp < 2 and q == 0:
+            acc[m] = out
+        else:
+            put[u](m, out + acc[m] if grp < 2 else out)
+
+    def run(u, store=None, post=None):
+        if u < 5:
+            pltpu.make_async_copy(s_buf.at[u], s_buf.at[u], s_sem.at[u]).wait()
+            pltpu.make_async_copy(n_buf.at[u], n_buf.at[u], n_sem.at[u]).wait()
+        if u > 0 and BLOCKS[u - 1][1] == 0:
+            basis[BLOCKS[u - 1][0]].wait()
+        for k in range(5):
+            if u > 0:
+                for m in ((0, 1), (2, 3), (4,), (), ())[k]:
+                    legendre(u - 1, m)
+            if u < 5:
+                advance(u, k)
+            if k == 2 and store is not None:
+                store()
+            if k == 3 and post is not None:
+                post()
+
+    def put_medium(m, out):
+        stage1[pl.ds(m, 128, stride=6), :] = out
 
     def put_first(m, out):
-        stage[pl.ds(m, 128, stride=10), :] = out
-
-    def put_medium(m, out):
-        stage[pl.ds(5 + m, 128, stride=10), :] = out
-
-    block(0, None)
+        if m < 4:
+            stage2[pl.ds(m, 128, stride=4), :] = out
+        else:
+            stage3[pl.ds(0, 128, stride=6), :] = out
+
+    def put_last(m, out):
+        stage3[pl.ds(1 + m, 128, stride=6), :] = out
+
+    def store1():
+        g1.reshape(768, 128)[...] = stage1[...].astype(BF16)
+
+    def store2():
+        g2.reshape(512, 128)[...] = stage2[...].astype(BF16)
+
+    put = {0: put_medium, 2: put_first, 4: put_last}
+    stage1[pl.ds(5, 128, stride=6), :] = jnp.zeros((128, 128), F32)
+    run(0)
     pl.semaphore_wait(barrier, ND - 1)
     send_all(me, c_msg, c_got, send.at[3], recv.at[3], here.at[3])
-    block(1, put_first)
-    block(2, put_medium)
-    g1.reshape(1280, 128)[...] = stage[...].astype(BF16)
-    block(3, None, lambda: send_all(me, g1, r1, send.at[0], recv.at[0], here.at[0]))
+    run(1, store1, lambda: send_all(me, g1, r1, send.at[0], recv.at[0], here.at[0]))
+    run(2)
+    run(3, store2, lambda: send_all(me, g2, r2, send.at[1], recv.at[1], here.at[1]))
+    run(4)
+    run(5)
+    g3.reshape(768, 128)[...] = stage3[...].astype(BF16)
+    send_all(me, g3, r3, send.at[2], recv.at[2], here.at[2])
 
     wait_rows(c_got, ND - 1, recv.at[3])
     pltpu.make_async_copy(c_got.at[me], c_got.at[me], here.at[3]).wait()
@@ -179,48 +206,19 @@
     part = [c_stage[pl.ds(k, 128, stride=4), :].astype(BF16) for k in range(4)]
     main = lax.dot_general(part[2], part[0], NT, preferred_element_type=F32)
     extra = lax.dot_general(part[3], part[1], NT, preferred_element_type=F32)
-    stage[pl.ds(5, 128, stride=6), :] = main + jnp.where(me < 32, extra, 0.0)
-    c_stage[pl.ds(0, 128, stride=2), :] = extra
-    c_stage[pl.ds(1, 128, stride=2), :] = jnp.zeros((128, 128), F32)
-    gx.reshape(256, 128)[...] = c_stage[pl.ds(0, 256), :].astype(BF16)
-    wide = jnp.logical_and(me >= 32, me < 64)
-    slot = lax.rem(me, 32)
-
-    def send_extra():
-        @pl.when(wide)
-        def _():
-            pltpu.make_async_copy(gx.at[me], rx.at[slot], here.at[4]).start()
-
-            def one(d):
-                pltpu.make_async_remote_copy(
-                    gx.at[d], rx.at[slot], send.at[4], recv.at[4], device_id=d, device_id_type=LOGICAL
-                ).start()
-
-            others(me, one)
-
-    def put_last(m, out):
-        stage[pl.ds(m, 128, stride=6), :] = out
-
-    block(4, put_last, send_extra)
-    g2.reshape(768, 128)[...] = stage[pl.ds(0, 768), :].astype(BF16)
-    send_all(me, g2, r2, send.at[1], recv.at[1], here.at[1])
+    c_stage[pl.ds(0, 128, stride=2), :] = main + jnp.where(me < 32, extra, 0.0)
+    c_stage[pl.ds(1, 128, stride=2), :] = extra
+    gc.reshape(256, 128)[...] = c_stage[pl.ds(0, 256), :].astype(BF16)
+    send_all(me, gc, rc, send.at[4], recv.at[4], here.at[4])
 
     wait_rows(c_got, ND - 1, send.at[3])
-
-    @pl.when(wide)
-    def _():
-        pltpu.make_async_copy(gx.at[0], rx.at[0], here.at[4]).wait()
-        wait_rows(gx, ND - 1, send.at[4])
-        wait_rows(rx, 31, recv.at[4])
-
-    @pl.when(jnp.logical_not(wide))
-    def _():
-        wait_rows(rx, 32, recv.at[4])
-
-    for k, r in enumerate((r1, r2)):
+    for k, r in enumerate((r1, r2, r3)):
         pltpu.make_async_copy(r.at[0], r.at[0], here.at[k]).wait()
         wait_rows(r, ND - 1, send.at[k])
         wait_rows(r, ND - 1, recv.at[k])
+    pltpu.make_async_copy(rc.at[0], rc.at[0], here.at[4]).wait()
+    wait_rows(rc, ND - 1, send.at[4])
+    wait_rows(rc, ND - 1, recv.at[4])
 
 
 def spectral_call(fs, fn, ms, mn, fb, mb, cs, cn, cb, dec, amp):
@@ -232,21 +230,25 @@
         out_shape=(
             v((5, 3200, 128), F32),
             v((1, 2, MC, MC), F32),
-            v((ND, 5, 2, 128), BF16),
             v((ND, 3, 2, 128), BF16),
-            v((32, 2, 128), BF16),
+            v((ND, 2, 2, 128), BF16),
+            v((ND, 3, 2, 128), BF16),
+            v((ND, 2, 128), BF16),
         ),
-        in_specs=[HBM] * 9 + [SMEM] * 2,
-        out_specs=(VMEM,) * 5,
+        in_specs=[HBM] * 11,
+        out_specs=(VMEM,) * 6,
         scratch_shapes=[
             v((5, 320, 5, 2, 128), BF16),
-            v((80, 128), BF16),
+            v((640, 128), BF16),
             v((10, 128, MF), BF16),
             v((5, 128, MM), BF16),
-            v((5, 128, 640), BF16),
+            v((2, 5, 128, 640), BF16),
             v((5, 128, 128), F32),
-            v((1280, 128), F32),
-            v((ND, 5, 2, 128), BF16),
+            v((768, 128), F32),
+            v((512, 128), F32),
+            v((768, 128), F32),
+            v((ND, 3, 2, 128), BF16),
+            v((ND, 2, 2, 128), BF16),
             v((ND, 3, 2, 128), BF16),
             v((ND, 2, 128), BF16),
             v((1, 2, MC, MC), F32),
@@ -256,10 +258,12 @@
             v((512, 128), F32),
             v((ND, 4, 128), BF16),
             v((ND, 4, 128), BF16),
+            pltpu.SMEM((3,), F32),
+            pltpu.SMEM((3,), F32),
             dma((5,)),
             dma((5,)),
             dma((3,)),
-            dma((3,)),
+            dma((5,)),
             dma((5,)),
             dma((5,)),
             dma((5,)),
@@ -269,7 +273,7 @@
     )(fs, fn, ms, mn, fb, mb, cs, cn, cb, dec, amp)
 
 
-def synthesis_kernel(s_buf, c_next, r1, r2, rx, w, tw, fo, mo, co, pat, f1, f2, cf, x, y, pv, o_sem, c_sem, p_sem):
+def synthesis_kernel(s_buf, c_next, r1, r2, r3, rc, w, tw, fo, mo, co, pat, f1, f2, f3, fc, cf, x, y, pv, o_sem, c_sem, p_sem):
     for u, (grp, q) in enumerate(BLOCKS):
         for kt in range(5):
             rows = s_buf.at[u].reshape(5 * 64, 5, 2, 128).at[pl.ds(kt * 64, 64)]
@@ -278,17 +282,18 @@
     coarse_out = pltpu.make_async_copy(c_next, co, c_sem)
     coarse_out.start()
 
-    f1[...] = r1.reshape(1280, 128)[...].astype(F32)
-    f2[...] = r2.reshape(768, 128)[...].astype(F32)
-    cf[pl.ds(0, 128), :] = f2[pl.ds(5, 128, stride=6), :]
-    y[pl.ds(0, 64), pl.ds(0, 128)] = rx.reshape(64, 128)[...].astype(F32)
-    cf[pl.ds(128, 32), :] = y[pl.ds(0, 64), pl.ds(0, 128)].reshape(32, 2, 128)[:, 0, :]
+    f1[...] = r1.reshape(768, 128)[...].astype(F32)
+    f2[...] = r2.reshape(512, 128)[...].astype(F32)
+    f3[...] = r3.reshape(768, 128)[...].astype(F32)
+    fc[...] = rc.reshape(256, 128)[...].astype(F32)
+    cf[pl.ds(0, 128), :] = fc[pl.ds(0, 128, stride=2), :]
+    cf[pl.ds(128, 32), :] = fc[pl.ds(65, 32, stride=2), :]
     for i in range(10):
-        if i < 5:
-            f = f1[pl.ds(i, 128, stride=10), :]
+        if i < 4:
+            f = f2[pl.ds(i, 128, stride=4), :]
         else:
-            f = f2[pl.ds(i - 5, 128, stride=6), :]
-        med = f1[pl.ds(5 + i % 5 + 10 * (i // 5), 64, stride=20), :]
+            f = f3[pl.ds(i - 4, 128, stride=6), :]
+        med = f1[pl.ds(i % 5 + 6 * (i // 5), 64, stride=12), :]
         coarse = cf[pl.ds(i, 16, stride=10), :]
         f = jnp.concatenate([f[:16] + (med[:16] + coarse), f[16:64] + med[16:], f[64:]], axis=0)
         if i == 0:
@@ -342,11 +347,13 @@
             s((1, 2, MC, MC), F32),
             s((NE, 1, NLON), F32),
         ),
-        in_specs=[VMEM] * 7,
+        in_specs=[VMEM] * 8,
         out_specs=(HBM,) * 4,
         scratch_shapes=[
-            v((1280, 128), F32),
             v((768, 128), F32),
+            v((512, 128), F32),
+            v((768, 128), F32),
+            v((256, 128), F32),
             v((160, 128), F32),
             v((640, 256), BF16),
             v((640, 512), F32),
@@ -362,8 +369,8 @@
 
 def body(fs, fn, ms, mn, cs, cn, decay, amplitude, fb, mb, cb):
     fs, fn, ms, mn = (a.transpose(0, 2, 1, 3) for a in (fs, fn, ms, mn))
-    big = [pltpu.with_memory_space_constraint(a, pltpu.HBM) for a in (fs, fn, ms, mn, fb, mb, cs, cn, cb)]
-    parts = spectral_call(*big, decay, amplitude)
+    big = [pltpu.with_memory_space_constraint(a, pltpu.HBM) for a in (fs, fn, ms, mn, fb, mb, cs, cn, cb, decay, amplitude)]
+    parts = spectral_call(*big)
     fine_next, medium_next, coarse_next, pattern = synthesis_call(*parts)
     return (fine_next.transpose(0, 2, 1, 3), medium_next.transpose(0, 2, 1, 3), coarse_next, pattern)
 

time: 32.6 us -> 29.8 us (0.914)
  Pallas kernels: 30.5 us -> 29.1 us
  local copies, waits for them, and re-layouts: 1.31 us -> 0.01 us
    pallas_call x1, Pallas kernels: 27 us -> 25.5 us  [spectral_call(): pl.pallas_call(spectral_kernel, name='spectral', out_shape=(v((5, 3200, 1...]
    unnamed x8 -> x4, local copies, waits for them, and re-layouts: 1.31 us -> 0.01 us
where the time goes in v4:
time: 29.8 us; the launch traced here: 29.7 us
  Pallas kernels  29.1 us (98%)
  between operations  0.67 us (2%)
    pallas_call x1, Pallas kernels, spectral_call(): pl.pallas_call(spectral_kernel, name='spectral', out_shape=(v((5, 3200, 1...  25.5 us
    pallas_call x1, Pallas kernels, synthesis_call(): pl.pallas_call(synthesis_kernel, name='synthesis', out_shape=(s((NE, 10,...  3.5 us

profile of v4, /device:TPU:1, one launch (start us, length us, event | category | flops | bytes accessed | tf_op | source)
XLA Modules:
  0.0 29.7 jit_solution(14771706110376192827)
XLA Ops:
  0.6 0.0 copy-start
  0.6 0.0 copy-start.1
  0.7 25.5 %spectral.1 = (f32[5,3200,128]{2,1,0:T(8,128)S(1)}, f32[1,2,160,160]{3,2,1,0:T(8,128)S(1)}, bf16[128,3,2,128]{3,2,1,0:T(2,128)(2,1)S(1)}, bf16[128,2,2,128]{3,2,...) custom-call(f32[64,10,2,1280]{3,2,1,0:T(2,128)} %bitcast.6, ...), custom_call_target="tpu_custom_call" | custom-call | flops 1000000000 | bytes 25000000 | tf_op jit(solution)/shard_map/spectral/pallas_call | solution.py:227
  26.2 0.0 copy-done
  26.2 0.0 copy-done.1
  26.2 3.5 %synthesis.1 = (f32[64,10,2,1280]{3,2,1,0:T(2,128)}, f32[64,5,2,640]{3,2,1,0:T(2,128)}, f32[1,2,160,160]{3,2,1,0:T(8,128)}, f32[64,1,2560]{2,1,0:T(1,128)}) custom-call(f32[5,3200,128]{2,1,0:T(8,128)S(1)} %get-tuple-element.14.s_buf, f32[1,2,160,160]{3,2,1,0:T(8,128)S(1)} %get-tuple-element.15.c_next, bf16[128,3,2,128]{3,2,1,0:T(2,128)(2,1)S(1)} %get-tuple-element.16.r1, ...), custom_call_target="tpu_custom_call" | custom-call | flops 100000000 | bytes 10000000 | tf_op jit(solution)/shard_map/synthesis/pallas_call | solution.py:341
Async XLA Ops:
  0.6 25.6 %copy-start = (bf16[256,512]{1,0:T(8,128)(2,1)S(1)}, bf16[256,512]{1,0:T(8,128)(2,1)}, u32[]{:S(2)}) copy-start(bf16[256,512]{1,0:T(8,128)(2,1)} %constant.4.clone.w) | copy-start | bytes 786436
  0.6 25.6 %copy-start.1 = (f32[32,1280]{1,0:T(8,128)S(1)}, f32[32,1280]{1,0:T(8,128)}, u32[]{:S(2)}) copy-start(f32[32,1280]{1,0:T(8,128)} %constant.5.clone.tw) | copy-start | bytes 491524

commit v5 on v4

--- a/solution.py
+++ b/solution.py
@@ -24,7 +24,7 @@
 BLOCKS = [(2, 0), (0, 0), (0, 1), (1, 0), (1, 1)]
 
 
-def others(act):
+def targets():
     lat = lax.axis_index("lat")
     y = lax.axis_index("scale") * 2 + lax.rem(lax.div(lat, 2), 2)
     x, z, core = lax.div(lat, 16), lax.rem(lax.div(lat, 4), 4), lax.rem(lat, 2)
@@ -33,26 +33,45 @@
         for dc in (1, 0):
             yy = lax.rem(y + dy, 4)
             low.append(lax.div(yy, 2) * 64 + lax.rem(yy, 2) * 2 + lax.rem(core + dc, 2))
-
-    @pl.loop(0, 15)
-    def _(t):
-        high = lax.rem(x + 1 + lax.div(t, 4), 4) * 16 + lax.rem(z + 1 + t, 4) * 4
-        for part in low:
-            act(high + part)
+    return x, z, low
+
+
+def others(act):
+    x, z, low = targets()
+    for dx in (2, 1, 3, 0):
+        xx = lax.rem(x + dx, 4) * 16
+
+        @pl.loop(1, 5 if dx else 4)
+        def _(t):
+            high = xx + lax.rem(z + t, 4) * 4
+            for part in low:
+                act(high + part)
 
     for part in low[:-1]:
         act(x * 16 + z * 4 + part)
 
 
-def send_all(me, src, dst, send, recv, here):
-    pltpu.make_async_copy(src.at[me], dst.at[me], here).start()
-
+def some_others(act, k):
+    x, z, low = targets()
+    pairs = [(dx, dz) for dx in (2, 1, 3, 0) for dz in (2, 1, 3, 0)]
+    for dx, dz in pairs[3 * k : 3 * k + 3 if k < 4 else 16]:
+        high = lax.rem(x + dx, 4) * 16 + lax.rem(z + dz, 4) * 4
+        for part in low if dx or dz else low[:-1]:
+            act(high + part)
+
+
+def send_all(me, src, dst, send, recv, here, k=None):
     def one(d):
         pltpu.make_async_remote_copy(
             src.at[d], dst.at[me], send, recv, device_id=d, device_id_type=LOGICAL
         ).start()
 
-    others(one)
+    if k is None or k == 0:
+        pltpu.make_async_copy(src.at[me], dst.at[me], here).start()
+    if k is None:
+        others(one)
+    else:
+        some_others(one, k)
 
 
 def wait_rows(ref, count, sem):
@@ -152,13 +171,15 @@
         else:
             put[u](m, out + acc[m] if grp < 2 else out)
 
-    def run(u, store=None, post=None):
+    def run(u, store=None, sends=None):
         if u < 5:
             pltpu.make_async_copy(s_buf.at[u], s_buf.at[u], s_sem.at[u]).wait()
             pltpu.make_async_copy(n_buf.at[u], n_buf.at[u], n_sem.at[u]).wait()
         if u > 0 and BLOCKS[u - 1][1] == 0:
             basis[BLOCKS[u - 1][0]].wait()
         for k in range(5):
+            if sends is not None:
+                sends(k)
             if u > 0:
                 for m in ((0, 1), (2, 3), (4,), (), ())[k]:
                     legendre(u - 1, m)
@@ -166,8 +187,6 @@
                 advance(u, k)
             if k == 2 and store is not None:
                 store()
-            if k == 3 and post is not None:
-                post()
 
     def put_medium(m, out):
         stage1[pl.ds(m, 128, stride=6), :] = out
@@ -190,12 +209,12 @@
     put = {0: put_medium, 2: put_first, 4: put_last}
     stage1[pl.ds(5, 128, stride=6), :] = jnp.zeros((128, 128), F32)
     run(0)
+    run(1, store1)
     pl.semaphore_wait(barrier, ND - 1)
     send_all(me, c_msg, c_got, send.at[3], recv.at[3], here.at[3])
-    run(1, store1, lambda: send_all(me, g1, r1, send.at[0], recv.at[0], here.at[0]))
-    run(2)
-    run(3, store2, lambda: send_all(me, g2, r2, send.at[1], recv.at[1], here.at[1]))
-    run(4)
+    run(2, None, lambda k: send_all(me, g1, r1, send.at[0], recv.at[0], here.at[0], k))
+    run(3, store2)
+    run(4, None, lambda k: send_all(me, g2, r2, send.at[1], recv.at[1], here.at[1], k))
     run(5)
     g3.reshape(768, 128)[...] = stage3[...].astype(BF16)
     send_all(me, g3, r3, send.at[2], recv.at[2], here.at[2])

time: 29.8 us -> 29.1 us (0.977)
  Pallas kernels: 29.1 us -> 28.3 us
    pallas_call x1, Pallas kernels: 25.5 us -> 24.8 us  [spectral_call(): pl.pallas_call(spectral_kernel, name='spectral', out_shape=(v((5, 3200, 1...]
where the time goes in v5:
time: 29.1 us; the launch traced here: 29 us
  Pallas kernels  28.3 us (97%)
  between operations  0.67 us (2%)
    pallas_call x1, Pallas kernels, spectral_call(): pl.pallas_call(spectral_kernel, name='spectral', out_shape=(v((5, 3200, 1...  24.8 us
    pallas_call x1, Pallas kernels, synthesis_call(): pl.pallas_call(synthesis_kernel, name='synthesis', out_shape=(s((NE, 10,...  3.5 us

profile of v5, /device:TPU:1, one launch (start us, length us, event | category | flops | bytes accessed | tf_op | source)
XLA Modules:
  0.0 29.0 jit_solution(16644465534123528766)
XLA Ops:
  0.6 0.0 copy-start
  0.6 0.0 copy-start.1
  0.7 24.8 %spectral.1 = (f32[5,3200,128]{2,1,0:T(8,128)S(1)}, f32[1,2,160,160]{3,2,1,0:T(8,128)S(1)}, bf16[128,3,2,128]{3,2,1,0:T(2,128)(2,1)S(1)}, bf16[128,2,2,128]{3,2,...) custom-call(f32[64,10,2,1280]{3,2,1,0:T(2,128)} %bitcast.6, ...), custom_call_target="tpu_custom_call" | custom-call | flops 1000000000 | bytes 25000000 | tf_op jit(solution)/shard_map/spectral/pallas_call | solution.py:246
  25.5 0.0 copy-done
  25.5 0.0 copy-done.1
  25.5 3.5 %synthesis.1 = (f32[64,10,2,1280]{3,2,1,0:T(2,128)}, f32[64,5,2,640]{3,2,1,0:T(2,128)}, f32[1,2,160,160]{3,2,1,0:T(8,128)}, f32[64,1,2560]{2,1,0:T(1,128)}) custom-call(f32[5,3200,128]{2,1,0:T(8,128)S(1)} %get-tuple-element.14.s_buf, f32[1,2,160,160]{3,2,1,0:T(8,128)S(1)} %get-tuple-element.15.c_next, bf16[128,3,2,128]{3,2,1,0:T(2,128)(2,1)S(1)} %get-tuple-element.16.r1, ...), custom_call_target="tpu_custom_call" | custom-call | flops 100000000 | bytes 10000000 | tf_op jit(solution)/shard_map/synthesis/pallas_call | solution.py:360
Async XLA Ops:
  0.6 24.8 %copy-start = (bf16[256,512]{1,0:T(8,128)(2,1)S(1)}, bf16[256,512]{1,0:T(8,128)(2,1)}, u32[]{:S(2)}) copy-start(bf16[256,512]{1,0:T(8,128)(2,1)} %constant.4.clone.w) | copy-start | bytes 786436
  0.6 24.8 %copy-start.1 = (f32[32,1280]{1,0:T(8,128)S(1)}, f32[32,1280]{1,0:T(8,128)}, u32[]{:S(2)}) copy-start(f32[32,1280]{1,0:T(8,128)} %constant.5.clone.tw) | copy-start | bytes 491524

commit v6 on v5

--- a/solution.py
+++ b/solution.py
@@ -211,9 +211,8 @@
     run(0)
     run(1, store1)
     pl.semaphore_wait(barrier, ND - 1)
-    send_all(me, c_msg, c_got, send.at[3], recv.at[3], here.at[3])
-    run(2, None, lambda k: send_all(me, g1, r1, send.at[0], recv.at[0], here.at[0], k))
-    run(3, store2)
+    run(2, None, lambda k: send_all(me, c_msg, c_got, send.at[3], recv.at[3], here.at[3], k))
+    run(3, store2, lambda k: send_all(me, g1, r1, send.at[0], recv.at[0], here.at[0], k))
     run(4, None, lambda k: send_all(me, g2, r2, send.at[1], recv.at[1], here.at[1], k))
     run(5)
     g3.reshape(768, 128)[...] = stage3[...].astype(BF16)

time: 29.1 us -> 29.2 us (level)
  no operation moved by 1% of the time
where the time goes in v6:
time: 29.2 us; the launch traced here: 29.1 us
  Pallas kernels  28.4 us (97%)
  between operations  0.67 us (2%)
    pallas_call x1, Pallas kernels, spectral_call(): pl.pallas_call(spectral_kernel, name='spectral', out_shape=(v((5, 3200, 1...  24.9 us
    pallas_call x1, Pallas kernels, synthesis_call(): pl.pallas_call(synthesis_kernel, name='synthesis', out_shape=(s((NE, 10,...  3.5 us

profile of v6, /device:TPU:1, one launch (start us, length us, event | category | flops | bytes accessed | tf_op | source)
XLA Modules:
  0.0 29.1 jit_solution(10394026192243532579)
XLA Ops:
  0.6 0.0 copy-start
  0.6 0.0 copy-start.1
  0.7 24.9 %spectral.1 = (f32[5,3200,128]{2,1,0:T(8,128)S(1)}, f32[1,2,160,160]{3,2,1,0:T(8,128)S(1)}, bf16[128,3,2,128]{3,2,1,0:T(2,128)(2,1)S(1)}, bf16[128,2,2,128]{3,2,...) custom-call(f32[64,10,2,1280]{3,2,1,0:T(2,128)} %bitcast.6, ...), custom_call_target="tpu_custom_call" | custom-call | flops 1000000000 | bytes 25000000 | tf_op jit(solution)/shard_map/spectral/pallas_call | solution.py:245
  25.6 0.0 copy-done
  25.6 0.0 copy-done.1
  25.6 3.5 %synthesis.1 = (f32[64,10,2,1280]{3,2,1,0:T(2,128)}, f32[64,5,2,640]{3,2,1,0:T(2,128)}, f32[1,2,160,160]{3,2,1,0:T(8,128)}, f32[64,1,2560]{2,1,0:T(1,128)}) custom-call(f32[5,3200,128]{2,1,0:T(8,128)S(1)} %get-tuple-element.14.s_buf, f32[1,2,160,160]{3,2,1,0:T(8,128)S(1)} %get-tuple-element.15.c_next, bf16[128,3,2,128]{3,2,1,0:T(2,128)(2,1)S(1)} %get-tuple-element.16.r1, ...), custom_call_target="tpu_custom_call" | custom-call | flops 100000000 | bytes 10000000 | tf_op jit(solution)/shard_map/synthesis/pallas_call | solution.py:359
Async XLA Ops:
  0.6 25.0 %copy-start = (bf16[256,512]{1,0:T(8,128)(2,1)S(1)}, bf16[256,512]{1,0:T(8,128)(2,1)}, u32[]{:S(2)}) copy-start(bf16[256,512]{1,0:T(8,128)(2,1)} %constant.4.clone.w) | copy-start | bytes 786436
  0.6 25.0 %copy-start.1 = (f32[32,1280]{1,0:T(8,128)S(1)}, f32[32,1280]{1,0:T(8,128)}, u32[]{:S(2)}) copy-start(f32[32,1280]{1,0:T(8,128)} %constant.5.clone.tw) | copy-start | bytes 491524
